TPU v7x, 256 devices: a whole 4x4x8 slice. The times are simulated.
256 devices in a mesh: dp: 2 (over x_lo), fsdp: 16 (over x_hi, y, core), tensor: 8 (over z).
Axes of the slice: x: 4 (x_hi: 2, x_lo: 2; x = x_hi * 2 + x_lo), y: 4, z: 8, core: 2. Of those that a mesh axis runs over, the one named last changes fastest.
Arguments:
- hidden: bfloat16 [16384, 2048], P(('dp', 'fsdp'), 'tensor'), may hold values from -8 to 8
- norm_gain: bfloat16 [2048], P('tensor'), may hold values from 0.099609375 to 1.8984375
- head_weight: bfloat16 [2048, 32128], P('fsdp', 'tensor'), may hold values from -1 to 1
- token_ids: int32 [32, 512], P(('dp', 'fsdp')), may hold values from 0 to 32127
- lengths: int32 [32], P(('dp', 'fsdp')), may hold values from 128 to 512
- old_logp: float32 [32, 512], P(('dp', 'fsdp')), may hold values from -12.5 to -9.5
- advantages: float32 [32, 512], P(('dp', 'fsdp')), may hold values from -4 to 4
- rollout_logp: float32 [32, 512], P(('dp', 'fsdp'), 'tensor'), may hold values from -16 to -1
- rollout_row: int32 [32], P(('dp', 'fsdp')), may hold values from 0 to 31, each once
Outputs:
- new_logp: float32 [32, 512], P(('dp', 'fsdp'))
- token_loss: float32 [32, 512], P(('dp', 'fsdp'))
- summary: float32 [3], replicated
Inputs may be any that keep to these rules, and one draw needn't show every extreme that they name: `rollout_row`: every row 0 to 31 is named once.
All inputs are finite; a program needn't handle non-finite values.
Results may differ from a plain program's by a relative error of at most 0.0005.
The roundings to bfloat16 on the way count: a program that leaves them out, or rounds other values in their place, can miss the bound.
Values may be sent and summed in bfloat16 or wider, within the bound.
A program may use at most 128 MiB of HBM per device.

v0:
```python
import jax
import jax.numpy as jnp
from jax import lax
from jax.sharding import PartitionSpec as P

clip_eps = 0.2
kl_coef = 0.2
log_limit = 10.0
norm_eps = 1e-06


def copy_for_each(array, axis):
    copies = jnp.broadcast_to(array, (lax.axis_size(axis), *array.shape))
    return lax.all_to_all(copies, axis, split_axis=0, concat_axis=0, tiled=True)


def taken_together(array, axis):
    everything = copy_for_each(array, axis)
    return jnp.max(everything, axis=0)


def taken_together_2(array, axis):
    everything = copy_for_each(array, axis)
    return jnp.sum(everything, axis=0)


def in_one(arrays, axis):
    line, at, outs = (jnp.concatenate([a.reshape(-1) for a in arrays]), 0, [])
    so_far = taken_together_2(line, axis)
    for a in arrays:
        outs.append(so_far[at : at + a.size].reshape(a.shape))
        at += a.size
    return tuple(outs)


def joined_along(tiles, dim):
    lengths = list(tiles.shape[1:])
    lengths[dim] *= tiles.shape[0]
    return jnp.moveaxis(tiles, 0, dim).reshape(lengths)


def collect(array, axis, dim):
    return joined_along(copy_for_each(array, axis), dim)


def token_terms(new_logp, old_logp, advantages, ref_logp, live_mask, prob_square):
    shift = new_logp - old_logp
    prob_ratio = jnp.exp(jnp.clip(shift, -log_limit, log_limit))
    clipped = jnp.clip(prob_ratio, 1.0 - clip_eps, 1.0 + clip_eps)
    plain_term = prob_ratio * advantages
    bounded_term = clipped * advantages
    surrogate = jnp.minimum(plain_term, bounded_term)
    ref_gap = ref_logp - new_logp
    gap_clip = jnp.clip(ref_gap, -log_limit, log_limit)
    kl_term = jnp.exp(gap_clip) - gap_clip - 1.0
    token_loss = live_mask * (kl_coef * kl_term - surrogate)
    inside_gap = (jnp.abs(ref_gap) < log_limit).astype(jnp.float32)
    inside_ratio = (jnp.abs(shift) < log_limit).astype(jnp.float32)
    active_term = (plain_term <= bounded_term).astype(jnp.float32)
    grad_coef = live_mask * (
        kl_coef * (1.0 - jnp.exp(gap_clip)) * inside_gap
        - advantages * prob_ratio * active_term * inside_ratio
    )
    grad_square = grad_coef * grad_coef * (prob_square - 2.0 * jnp.exp(new_logp) + 1.0)
    return (token_loss, live_mask * kl_term, grad_square)


def exp_sums(logits, row_max):
    shifted = jnp.exp(logits - row_max[:, None])
    return (jnp.sum(shifted, axis=1), jnp.sum(shifted * shifted, axis=1))


def vocab_stats(logits, flat_ids, col_start):
    col_ids = lax.broadcasted_iota(jnp.int32, logits.shape, 1) + col_start
    picked = jnp.sum(jnp.where(col_ids == flat_ids[:, None], logits, 0.0), axis=1)
    local_max = jnp.max(logits, axis=1)
    row_max = taken_together(local_max, "tensor")
    exp_sum, exp_square = exp_sums(logits, row_max)
    exp_sum, exp_square, picked = in_one((exp_sum, exp_square, picked), "tensor")
    return (row_max, exp_sum, exp_square, picked)


def shards(
    hidden,
    norm_gain,
    head_weight,
    token_ids,
    lengths,
    old_logp,
    advantages,
    rollout_logp,
    rollout_row,
):
    full_rows, full_gain = (collect(hidden, "tensor", 1), collect(norm_gain, "tensor", 0))
    values = full_rows.astype(jnp.float32)
    inv_rms = lax.rsqrt(jnp.mean(values * values, axis=1, keepdims=True) + norm_eps)
    normed = (values * inv_rms * full_gain.astype(jnp.float32)[None, :]).astype(jnp.bfloat16)
    flat_ids = token_ids.reshape(-1)
    vocab_cols = head_weight.shape[1]
    tensor_pos = lax.axis_index("tensor")
    logits = jnp.dot(
        normed,
        lax.all_gather(head_weight, "fsdp", axis=0, tiled=True),
        preferred_element_type=jnp.float32,
    )
    soft_stats = vocab_stats(logits, flat_ids, tensor_pos * vocab_cols)
    row_max, exp_sum, exp_square, picked = soft_stats
    new_logp = (picked - row_max - jnp.log(exp_sum)).reshape(token_ids.shape)
    prob_square = (exp_square / (exp_sum * exp_sum)).reshape(token_ids.shape)
    ref_all = collect(rollout_logp, ("dp", "fsdp"), 0)
    own_ref = jnp.take(ref_all, rollout_row, axis=0)
    ref_logp = collect(own_ref, "tensor", 1)
    positions = lax.broadcasted_iota(jnp.int32, token_ids.shape, 1)
    live_mask = (positions < lengths[:, None]).astype(jnp.float32)
    token_loss, kl_part, grad_part = token_terms(
        new_logp, old_logp, advantages, ref_logp, live_mask, prob_square
    )
    live_count, loss_sum, kl_sum, grad_sum = in_one(
        (jnp.sum(live_mask), jnp.sum(token_loss), jnp.sum(kl_part), jnp.sum(grad_part)),
        ("dp", "fsdp"),
    )
    summary = jnp.stack(
        [loss_sum / live_count, kl_sum / live_count, jnp.sqrt(grad_sum / live_count)]
    )
    return (new_logp, token_loss, summary)


def solution(mesh):
    in_specs = (
        P(("dp", "fsdp"), "tensor"),
        P("tensor"),
        P("fsdp", "tensor"),
        P(("dp", "fsdp"), None),
        P(("dp", "fsdp")),
        P(("dp", "fsdp"), None),
        P(("dp", "fsdp"), None),
        P(("dp", "fsdp"), "tensor"),
        P(("dp", "fsdp")),
    )
    out_specs = (P(("dp", "fsdp"), None), P(("dp", "fsdp"), None), P())
    return jax.shard_map(shards, mesh=mesh, in_specs=in_specs, out_specs=out_specs, check_vma=False)
```

profile of v0, /device:TPU:1, one launch (start us, length us, event | category | flops | bytes accessed | tf_op | source)
XLA Modules:
  0.0 218.8 jit_solution(17460148132570036709)
XLA Ops:
  7.2 0.0 copy-start.4
  7.2 0.0 all-gather.2.cloned.1.call-start
  7.2 0.7 all-gather.2.cloned.1.call-update
  7.9 0.7 broadcast_in_dim.42
  8.6 0.5 broadcast.150
  9.1 0.7 reduce.12
  9.8 0.6 reshape.211
  10.4 9.0 %all-to-all-start.1 = ((bf16[8,2,128]{2,1,0:T(2,128)(2,1)}), bf16[8,2,128]{2,1,0:T(2,128)(2,1)S(1)}, u32[]{:S(2)}, u32[]{:S(2)}) async-start(bf16[8,2,128]{2,1,0:T(2,128)(2,1)} %reshape.211), calls=%async_computation.1 | async-start | bytes 8192 | tf_op jit(solution)/shard_map/all_to_all | solution.py:14
  19.4 1.1 copy.14
  20.5 5.5 %all-to-all-done.1 = bf16[8,2,128]{2,1,0:T(2,128)(2,1)S(1)} async-done(((bf16[8,2,128]{2,1,0:T(2,128)(2,1)}), bf16[8,2,128]{2,1,0:T(2,128)(2,1)S(1)}, u32[]{:S(2)}, u32[]{:S(2)}) %all-to-all-start.1) | async-done | bytes 4128 | tf_op jit(solution)/shard_map/all_to_all | solution.py:14
  25.9 1.5 broadcast_in_dim.41
  27.4 3.6 %all-to-all-start = ((bf16[8,512,256]{1,2,0:T(8,128)(2,1)}), bf16[8,512,256]{1,2,0:T(8,128)(2,1)S(1)}, u32[]{:S(2)}, u32[]{:S(2)}) async-start(bf16[8,512,256]{1,2,0:T(8,128)(2,1)} %broadcast_in_dim.41), calls=%async_computation | async-start | bytes 4194304 | tf_op jit(solution)/shard_map/all_to_all | solution.py:14
  31.8 50.9 %all-to-all-done = bf16[8,512,256]{1,2,0:T(8,128)(2,1)S(1)} async-done(((bf16[8,512,256]{1,2,0:T(8,128)(2,1)}), bf16[8,512,256]{1,2,0:T(8,128)(2,1)S(1)}, u32[]{:S(2)}, u32[]{:S(2)}) %all-to-all-start) | async-done | bytes 2097184 | tf_op jit(solution)/shard_map/all_to_all | solution.py:14
  82.6 0.0 copy-done.4
  82.6 0.6 broadcast_in_dim.48
  83.2 7.6 %all-to-all-start.4 = ((f32[32,1,64]{2,1,0:T(1,128)}), f32[32,1,64]{2,1,0:T(1,128)S(1)}, u32[]{:S(2)}, u32[]{:S(2)}) async-start(f32[32,1,64]{2,1,0:T(1,128)} %broadcast_in_dim.48), calls=%async_computation.4 | async-start | bytes 32768 | tf_op jit(solution)/shard_map/all_to_all | solution.py:14
  90.9 0.5 multiply_reduce_fusion.1
  91.4 2.0 fusion.2
  93.4 43.2 %all-gather.2.cloned.1.call-done = bf16[2048,4016]{0,1:T(8,128)(2,1)} async-done(((bf16[128,4016]{0,1:T(8,128)(2,1)}), bf16[2048,4016]{0,1:T(8,128)(2,1)}) %all-gather.2.cloned.1.call-update) | async-done | bytes 16449552 | tf_op jit(solution)/shard_map/all_gather | solution.py:103
  136.5 14.8 %fusion.18 = (f32[512]{0:T(512)S(1)}, f32[512,4016]{0,1:T(8,128)}) fusion(bf16[2048,4016]{0,1:T(8,128)(2,1)} %all-gather.2.cloned.1.call-done, bf16[512,2048]{0,1:T(8,128)(2,1)} %fusion.2), kind=kOutput, calls=%fused_computation.43 | convolution fusion | flops 8424218112 | bytes 26773504 | tf_op jit(solution)/shard_map/dot_general | solution.py:101
  151.3 0.0 all-to-all-done.4
  151.3 0.6 broadcast_in_dim.43
  151.9 6.7 %all-to-all-start.2 = ((f32[8,1,512]{2,1,0:T(1,128)}), f32[8,1,512]{2,1,0:T(1,128)S(1)}, u32[]{:S(2)}, u32[]{:S(2)}) async-start(f32[8,1,512]{2,1,0:T(1,128)} %broadcast_in_dim.43), calls=%async_computation.2 | async-start | bytes 32768 | tf_op jit(solution)/shard_map/all_to_all | solution.py:14
  158.7 6.6 %all-to-all-done.2 = f32[8,1,512]{2,1,0:T(1,128)S(1)} async-done(((f32[8,1,512]{2,1,0:T(1,128)}), f32[8,1,512]{2,1,0:T(1,128)S(1)}, u32[]{:S(2)}, u32[]{:S(2)}) %all-to-all-start.2) | async-done | bytes 16416 | tf_op jit(solution)/shard_map/all_to_all | solution.py:14
  165.3 0.6 broadcast_in_dim.50
  165.9 3.3 %all-to-all-start.5 = ((f32[8,1,64]{2,1,0:T(1,128)}), f32[8,1,64]{2,1,0:T(1,128)S(1)}, u32[]{:S(2)}, u32[]{:S(2)}) async-start(f32[8,1,64]{2,1,0:T(1,128)} %broadcast_in_dim.50), calls=%async_computation.5 | async-start | bytes 8192 | tf_op jit(solution)/shard_map/all_to_all | solution.py:14
  169.2 0.0 copy-done.3
  169.3 0.0 copy-start.1
  169.3 0.0 copy-start.2
  169.3 5.4 %fusion = (f32[512]{0:T(512)S(1)}, f32[512]{0:T(512)S(1)}, f32[512]{0:T(512)S(1)}) fusion(f32[512,4016]{0,1:T(8,128)} %get-tuple-element.29, f32[512]{0:T(512)S(1)} %reduce_max.19, s32[512]{0:T(512)S(1)} %bitcast.36, s32[4016]{0:T(1024)S(1)} %iota_add_fusion), kind=kLoop, calls=%fused_computation.3 | loop fusion | flops 14391808 | bytes 8251072 | tf_op jit(solution)/shard_map/reduce_sum | solution.py:70
  174.7 1.0 all-to-all-done.5
  175.7 0.6 broadcast_in_dim.45
  176.3 5.6 %all-to-all-start.3 = ((f32[8,1,1536]{2,1,0:T(1,128)}), f32[8,1,1536]{2,1,0:T(1,128)S(1)}, u32[]{:S(2)}, u32[]{:S(2)}) async-start(f32[8,1,1536]{2,1,0:T(1,128)} %broadcast_in_dim.45), calls=%async_computation.3 | async-start | bytes 98304 | tf_op jit(solution)/shard_map/all_to_all | solution.py:14
  182.6 0.5 broadcast.148
  183.1 0.7 reduce.11
  183.8 0.1 reshape_transpose.3
  183.9 5.1 %all-to-all-done.3 = f32[8,1,1536]{2,1,0:T(1,128)S(1)} async-done(((f32[8,1,1536]{2,1,0:T(1,128)}), f32[8,1,1536]{2,1,0:T(1,128)S(1)}, u32[]{:S(2)}, u32[]{:S(2)}) %all-to-all-start.3) | async-done | bytes 49184 | tf_op jit(solution)/shard_map/all_to_all | solution.py:14
  189.1 0.0 copy-start
  189.1 0.1 sub.73
  189.2 0.6 reduce_sum.97
  189.8 0.0 copy-done.1
  189.8 0.0 copy-done.2
  189.8 1.3 fusion.15
  191.1 2.6 %pad_maximum_fusion.1 = f32[4]{0:T(128)S(1)} fusion(f32[1]{0:T(128)} %bitcast.17, f32[1]{0:T(128)} %bitcast.14, f32[1]{0:T(128)} %bitcast.12, f32[1]{0:T(128)} %bitcast.11), kind=kLoop, calls=%fused_computation.38 | loop fusion | flops 12 | bytes 32 | tf_op jit(solution)/shard_map/concatenate | solution.py:28
  193.7 13.1 %all_to_all.39 = f32[32,1,4]{2,1,0:T(1,128)S(1)} all-to-all(f32[32,1,4]{2,1,0:T(1,128)S(1)} %broadcast_in_dim.51), channel_id=1, replica_groups=mesh['dp'=2,'fsdp'=16,'tensor'=8] {'dp','fsdp'}, dimensions={0} | all-to-all | bytes 1024 | tf_op jit(solution)/shard_map/all_to_all | solution.py:14
  206.8 0.1 reduce_sum.99
  206.9 0.7 fusion.17
  211.3 0.6 pad_maximum_fusion.2
  (14 shorter events, 0.2 us)
Async XLA Ops:
  7.2 75.5 %copy-start.4 = (f32[1,64]{1,0:T(1,128)S(1)}, f32[1,64]{1,0:T(1,128)}, u32[]{:S(2)}) copy-start(f32[1,64]{1,0:T(1,128)} %param.16) | copy-start | bytes 772
  7.2 129.3 %all-gather.2.cloned.1.call-start = ((), (), s32[]{:S(2)}) async-start(), calls=%async_computation.7 | async-start | bytes 17477632 | tf_op jit(solution)/shard_map/all_gather | solution.py:103
  10.4 15.6 %all-to-all-start.1 = ((bf16[8,2,128]{2,1,0:T(2,128)(2,1)}), bf16[8,2,128]{2,1,0:T(2,128)(2,1)S(1)}, u32[]{:S(2)}, u32[]{:S(2)}) async-start(bf16[8,2,128]{2,1,0:T(2,128)(2,1)} %reshape.211), calls=%async_computation.1 | async-start | bytes 8192 | tf_op jit(solution)/shard_map/all_to_all | solution.py:14
  27.4 55.2 %all-to-all-start = ((bf16[8,512,256]{1,2,0:T(8,128)(2,1)}), bf16[8,512,256]{1,2,0:T(8,128)(2,1)S(1)}, u32[]{:S(2)}, u32[]{:S(2)}) async-start(bf16[8,512,256]{1,2,0:T(8,128)(2,1)} %broadcast_in_dim.41), calls=%async_computation | async-start | bytes 4194304 | tf_op jit(solution)/shard_map/all_to_all | solution.py:14
  83.2 68.1 %all-to-all-start.4 = ((f32[32,1,64]{2,1,0:T(1,128)}), f32[32,1,64]{2,1,0:T(1,128)S(1)}, u32[]{:S(2)}, u32[]{:S(2)}) async-start(f32[32,1,64]{2,1,0:T(1,128)} %broadcast_in_dim.48), calls=%async_computation.4 | async-start | bytes 32768 | tf_op jit(solution)/shard_map/all_to_all | solution.py:14
  93.4 75.9 %copy-start.3 = (s32[1,512]{1,0:T(1,128)S(1)}, s32[1,512]{1,0:T(1,128)}, u32[]{:S(2)}) copy-start(s32[1,512]{1,0:T(1,128)} %param.12) | copy-start | bytes 6148
  151.9 13.4 %all-to-all-start.2 = ((f32[8,1,512]{2,1,0:T(1,128)}), f32[8,1,512]{2,1,0:T(1,128)S(1)}, u32[]{:S(2)}, u32[]{:S(2)}) async-start(f32[8,1,512]{2,1,0:T(1,128)} %broadcast_in_dim.43), calls=%async_computation.2 | async-start | bytes 32768 | tf_op jit(solution)/shard_map/all_to_all | solution.py:14
  165.9 9.8 %all-to-all-start.5 = ((f32[8,1,64]{2,1,0:T(1,128)}), f32[8,1,64]{2,1,0:T(1,128)S(1)}, u32[]{:S(2)}, u32[]{:S(2)}) async-start(f32[8,1,64]{2,1,0:T(1,128)} %broadcast_in_dim.50), calls=%async_computation.5 | async-start | bytes 8192 | tf_op jit(solution)/shard_map/all_to_all | solution.py:14
  169.3 20.6 %copy-start.1 = (f32[1,512]{1,0:T(1,128)S(1)}, f32[1,512]{1,0:T(1,128)}, u32[]{:S(2)}) copy-start(f32[1,512]{1,0:T(1,128)} %param.15) | copy-start | bytes 6148
  169.3 20.6 %copy-start.2 = (f32[1,512]{1,0:T(1,128)S(1)}, f32[1,512]{1,0:T(1,128)}, u32[]{:S(2)}) copy-start(f32[1,512]{1,0:T(1,128)} %param.14) | copy-start | bytes 6148
  176.3 12.7 %all-to-all-start.3 = ((f32[8,1,1536]{2,1,0:T(1,128)}), f32[8,1,1536]{2,1,0:T(1,128)S(1)}, u32[]{:S(2)}, u32[]{:S(2)}) async-start(f32[8,1,1536]{2,1,0:T(1,128)} %broadcast_in_dim.45), calls=%async_computation.3 | async-start | bytes 98304 | tf_op jit(solution)/shard_map/all_to_all | solution.py:14
  189.1 22.9 %copy-start = (f32[512]{0:T(512)}, f32[512]{0:T(512)S(1)}, u32[]{:S(2)}) copy-start(f32[512]{0:T(512)S(1)} %get-tuple-element.20) | copy-start | bytes 6148
Sparse Core Ops, SparseCore 0:
  10.5 125.9 all-gather.1
where the time goes:
time: 219 us
  waiting for transfers between devices  113 us (52%)
  starting transfers between devices  36 us (16%)
  between operations  19.3 us (9%)
  matrix products  14.8 us (7%)
  other arithmetic  14.5 us (7%)
  blocking collectives  13.1 us (6%)
  local copies, waits for them, and re-layouts  8.21 us (4%)
    all_to_all x6, waiting for transfers between devices, copy_for_each(): return lax.all_to_all(copies, axis, split_axis=0, concat_axis=0, tiled=True)  69 us
    all_gather x1, waiting for transfers between devices, shards(): lax.all_gather(head_weight, 'fsdp', axis=0, tiled=True)  43.2 us
    all_to_all x6, starting transfers between devices, copy_for_each(): return lax.all_to_all(copies, axis, split_axis=0, concat_axis=0, tiled=True)  35.9 us
    dot_general x1, matrix products, shards(): jnp.dot(normed, lax.all_gather(head_weight, 'fsdp', axis=0, tiled=True),...  14.8 us
    all_to_all x1, blocking collectives, copy_for_each(): return lax.all_to_all(copies, axis, split_axis=0, concat_axis=0, tiled=True)  13.1 us
    reduce_sum x1, other arithmetic, exp_sums(): return (jnp.sum(shifted, axis=1), jnp.sum(shifted * shifted, axis=1))  5.43 us
    broadcast_in_dim x8, local copies, waits for them, and re-layouts, copy_for_each(): copies = jnp.broadcast_to(array, (lax.axis_size(axis), *array.shape))  5.14 us
  transfers between devices with their start and end apart: 7, of which 6 were waited for; matrix products, arithmetic and copies ran while one was open for 14% of the time, Pallas kernels for 0%

commit v1 on v0

v1 whole, which is shorter than its diff:
```python
import functools
import heapq

import jax
import jax.numpy as jnp
from jax import lax
from jax.experimental import pallas as pl
from jax.experimental.pallas import tpu as pltpu
from jax.sharding import PartitionSpec as P

clip_eps = 0.2
kl_coef = 0.2
log_limit = 10.0
norm_eps = 1e-06

MESH = pl.DeviceIdType.MESH
LOW = -1e30
CHUNK = 256
SUB = 128
STEP = 256
DEPTH = 3


def through_y(pair):
    return pair % 2 == 1


def links_of(item, subs):
    out = []
    if item[0] == "w":
        _, col, dy, pair, r = item
        if col == 0:
            if dy == 0 or (dy == 3 and r == 0):
                out.append("yp")
            if dy == 0 or (dy == 1 and r == 1):
                out.append("ym")
            if r == 1 and not (dy == 2 and through_y(pair)):
                out.append("h")
        else:
            if r == 0 and not (dy == 2 and through_y(pair)):
                out.append("l")
            if through_y(pair) and (dy, r) == (3, 0):
                out.append("yp")
            if through_y(pair) and (dy, r) == (1, 1):
                out.append("ym")
    else:
        _, dz, sub = item
        first = sub < subs // 2
        if dz in (0, 7, 6) or (dz == 5 and first):
            out.append("zp")
        if dz in (0, 1, 2) or (dz == 3 and not first):
            out.append("zm")
    return out


def arrives_as(link, item):
    if item[0] == "w":
        _, col, dy, pair, r = item
        if link == "yp":
            return ("w", col, (dy - 1) % 4, pair, r)
        if link == "ym":
            return ("w", col, (dy + 1) % 4, pair, r)
        if link == "h":
            return ("w", 1 - col, dy, pair, 1 - r)
        return ("w", col, dy, pair, 1 - r)
    return ("h", (item[1] + (-1 if link == "zp" else 1)) % 8, item[2])


def rank(link, item):
    if item[0] == "w":
        return (item[3], item[2] != 0 if link[0] == "y" else 0, item[1], item[4])
    return (min(item[1], 8 - item[1]) + item[2] / 4, item[2])


def plan(pairs, subs):
    wire = {"w": 2.85, "h": 1.45}
    delay, norm_time, chunk_time, own_time = 2.0, 0.8, 1.4, 2.0
    names = ("zp", "zm", "yp", "ym", "h", "l")
    free = dict.fromkeys(names, 0.0)
    ends = {n: [] for n in names}
    ready = {n: [] for n in names}
    arrivals, ops = [], []
    for sub in range(subs):
        heapq.heappush(arrivals, (0.0, ("h", 0, sub)))
    for pair in range(pairs):
        for r in (0, 1):
            heapq.heappush(arrivals, (own_time, ("w", 0, 0, pair, r)))
    missing = {("c", pair, r): 8 for pair in range(pairs) for r in (0, 1)}
    missing.update({("n", sub): 8 for sub in range(subs)})
    tokens_missing, normable, computable = 2 * subs, [], []
    now = 0.0

    def top_up():
        for n in names:
            ends[n] = [e for e in ends[n] if e > now]
            while ready[n] and len(ends[n]) < DEPTH:
                _, item = heapq.heappop(ready[n])
                end = max(now, free[n]) + wire[item[0]]
                free[n] = end
                ends[n].append(end)
                ops.append(("send", n, item))
                heapq.heappush(arrivals, (end + delay, arrives_as(n, item)))

    while arrivals or normable or computable:
        if arrivals and arrivals[0][0] <= now:
            _, item = heapq.heappop(arrivals)
            own = item[0] == "h" and item[1] == 0 or item[0] == "w" and item[1:3] == (0, 0)
            if not own or item[0] == "w" and item[3:] == (0, 0) or item == ("h", 0, 0):
                ops.append(("wait", item))
            if item[0] == "p":
                tokens_missing -= 1
                continue
            for n in links_of(item, subs):
                heapq.heappush(ready[n], (rank(n, item), item))
            if not own or not arrivals or arrivals[0][0] > now:
                top_up()
            key = ("c", *item[3:]) if item[0] == "w" else ("n", item[2])
            missing[key] -= 1
            if missing[key] == 0:
                (computable if key[0] == "c" else normable).append(key)
        elif normable:
            key = normable.pop(0)
            now += norm_time
            ops.append(("norm", key[1]))
            tokens_missing -= 1
            heapq.heappush(arrivals, (now + 1.8, ("p", key[1])))
            top_up()
        elif computable and tokens_missing == 0:
            key = computable.pop(0)
            now += chunk_time
            ops.append(("chunk", *key[1:]))
            top_up()
        else:
            now = max(now, arrivals[0][0])
            top_up()
    return ops, now


def kernel(
    hidden, gain, weight, ids, lens, old, adv, roll, row,
    logp_out, loss_out, sum_out,
    w_all, w_own, w_send, hid, normed, id_peer, id_cols, m_acc, s_acc, q_acc, p_acc,
    stat_rows, stat_peer, stat_all, ref_rows, ref_all, gains, tot_all,
    local_sem, w_sem, h_sem, n_sem, g_sem, r_sem, z_sem, s_sem, t_sem, pair_sem, send_sem,
):
    lo, f, z = lax.axis_index("dp"), lax.axis_index("fsdp"), lax.axis_index("tensor")
    hi, y, c = f // 8, (f // 2) % 4, f % 2
    me = lo * 16 + f
    subs = hid.shape[1] // SUB
    chunks = w_all.shape[0]
    rows_dev, cols = weight.shape
    half = chunks * CHUNK
    own_tokens = ids.shape[1]
    zs = stat_all.shape[0]
    blocks = own_tokens // 128

    def at(hi_, lo_, y_, c_, z_):
        return {"dp": lo_, "fsdp": hi_ * 8 + y_ * 2 + c_, "tensor": z_}

    partner = at(hi, lo, y, 1 - c, z)
    target = {
        "yp": at(hi, lo, (y + 1) % 4, c, z),
        "ym": at(hi, lo, (y + 3) % 4, c, z),
        "h": at(1 - hi, 1 - lo, y, c, z),
        "l": at(hi, 1 - lo, y, c, z),
        "zp": at(hi, lo, y, c, (z + 1) % zs),
        "zm": at(hi, lo, y, c, (z + zs - 1) % zs),
    }

    def plane_peer(k):
        other = (me + k) % 32
        return {"dp": other // 16, "fsdp": other % 16, "tensor": z}

    def line_peer(k):
        return {"dp": lo, "fsdp": f, "tensor": (z + k) % zs}

    def remote(src, dst, s, r, device):
        return pltpu.make_async_remote_copy(
            src_ref=src, dst_ref=dst, send_sem=s, recv_sem=r, device_id=device, device_id_type=MESH
        )

    hid_in = pltpu.make_async_copy(hidden, hid.at[z], local_sem.at[0])
    w_in = pltpu.make_async_copy(weight, w_own, local_sem.at[1])
    w_in.start()
    hid_in.start()

    barrier = pltpu.get_barrier_semaphore()

    @pl.loop(1, 32)
    def _(k):
        pl.semaphore_signal(barrier, inc=1, device_id=plane_peer(k), device_id_type=MESH)

    @pl.loop(1, zs)
    def _(k):
        pl.semaphore_signal(barrier, inc=1, device_id=line_peer(k), device_id_type=MESH)

    lane = lax.broadcasted_iota(jnp.int32, (1, 128), 1)
    group = hi * 4 + y
    row0 = pl.multiple_of(group * 256 + c * rows_dev, rows_dev)
    gains[z] = gain[...].astype(jnp.float32)
    own_roll = roll[...]
    ref_rows[me] = jnp.concatenate([own_roll, own_roll], axis=1)
    w_in.wait()

    def split(own):
        for side in (own, 1 - own):
            for j in range(chunks):
                start = side * half + j * CHUNK
                width = min(CHUNK, cols - start)
                if width < CHUNK:
                    if side == own:
                        w_all[j, pl.ds(row0, rows_dev), :] = jnp.zeros((rows_dev, CHUNK), jnp.bfloat16)
                    else:
                        w_send[j] = jnp.zeros((rows_dev, CHUNK), jnp.bfloat16)
                piece = w_own[:, start : start + width]
                if side == own:
                    w_all[j, pl.ds(row0, rows_dev), :width] = piece
                else:
                    w_send[j, :, :width] = piece

    @pl.when(c == 0)
    def _():
        split(0)

    @pl.when(c == 1)
    def _():
        split(1)

    hid_in.wait()
    pl.semaphore_wait(barrier, 31 + zs - 1)

    id_copy = remote(ids, id_peer, send_sem.at[0], pair_sem.at[0], partner)
    w_pair = remote(w_send, w_all.at[:, pl.ds(row0, rows_dev), :], send_sem.at[1], pair_sem.at[1], partner)

    def w_piece(col, dy, pair, r):
        g = (1 - hi if col else hi) * 4 + (y + dy) % 4
        j = 2 * pair + (1 - lo if r else lo)
        return w_all.at[j, pl.ds(pl.multiple_of(g * 256, 256), 256), :], w_sem.at[g, j]

    def h_piece(dz, sub):
        owner = (z + dz) % zs
        return hid.at[owner, pl.ds(sub * SUB, SUB), :], h_sem.at[owner, sub]

    def move(link, item):
        if item[0] == "w":
            ref, sem = w_piece(*item[1:])
            return remote(ref, ref, send_sem.at[2], sem, target[link])
        ref, sem = h_piece(*item[1:])
        return remote(ref, ref, send_sem.at[3], sem, target[link])

    def token_rows(core, sub):
        return normed.at[pl.ds(pl.multiple_of(core * own_tokens + sub * SUB, SUB), SUB), :]

    def normalize(sub):
        @pl.loop(0, SUB // 32)
        def _(t):
            rows = pl.ds(pl.multiple_of(sub * SUB + t * 32, 32), 32)
            squares = jnp.zeros((32, 1), jnp.float32)
            for k in range(zs):
                part = hid[k, rows, :].astype(jnp.float32)
                squares += jnp.sum(part * part, axis=1, keepdims=True)
            inv = lax.rsqrt(squares * (1.0 / (zs * hid.shape[2])) + norm_eps)
            out = pl.ds(pl.multiple_of(c * own_tokens + sub * SUB + t * 32, 32), 32)
            for k in range(zs):
                part = hid[k, rows, :].astype(jnp.float32)
                width = hid.shape[2]
                normed[out, k * width : (k + 1) * width] = (part * inv * gains[k]).astype(jnp.bfloat16)

    def pair_tokens(sub):
        ref = token_rows(c, sub)
        return remote(ref, ref, send_sem.at[4], n_sem.at[sub], partner)

    def chunk(j):
        base = c * half + j * CHUNK

        @pl.loop(0, normed.shape[0] // STEP)
        def _(t):
            rows = pl.ds(pl.multiple_of(t * STEP, STEP), STEP)
            logits = jnp.dot(normed[rows, :], w_all[j], preferred_element_type=jnp.float32)
            col_a = base + lax.broadcasted_iota(jnp.int32, (STEP, 128), 1)
            wanted = id_cols[rows, :]
            a = jnp.where(col_a < cols, logits[:, :128], LOW)
            b = jnp.where(col_a < cols - 128, logits[:, 128:], LOW)
            where = wanted - col_a.astype(jnp.float32)
            p_acc[rows, :] += jnp.where(where == 0.0, a, 0.0) + jnp.where(where == 128.0, b, 0.0)
            old_max = m_acc[rows, :]
            new_max = jnp.maximum(old_max, jnp.maximum(a, b))
            scale = jnp.exp(old_max - new_max)
            exp_a, exp_b = jnp.exp(a - new_max), jnp.exp(b - new_max)
            s_acc[rows, :] = s_acc[rows, :] * scale + (exp_a + exp_b)
            q_acc[rows, :] = q_acc[rows, :] * (scale * scale) + (exp_a * exp_a + exp_b * exp_b)
            m_acc[rows, :] = new_max

    def ref_start():
        @pl.loop(1, 32)
        def _(k):
            remote(ref_rows.at[me], ref_rows.at[me], send_sem.at[5], r_sem.at[k], plane_peer(k)).start()

    def ref_pick():
        @pl.loop(1, 32)
        def _(k):
            src = ref_rows.at[(me + 32 - k) % 32]
            remote(src, src, send_sem.at[5], r_sem.at[k], partner).wait_recv()

        ref_all[z] = ref_rows[row[0]]

    def ref_send():
        @pl.loop(1, zs)
        def _(k):
            remote(ref_all.at[z], ref_all.at[z], send_sem.at[6], z_sem.at[k], line_peer(k)).start()

    def ref_wait():
        @pl.loop(1, zs)
        def _(k):
            src = ref_all.at[(z + zs - k) % zs]
            remote(src, src, send_sem.at[6], z_sem.at[k], partner).wait_recv()

    def ids_to_columns():
        remote(ids, id_peer, send_sem.at[0], pair_sem.at[0], partner).wait_recv()
        for b in range(2 * blocks):
            source = ids if b < blocks else id_peer
            line = source[:, (b % blocks) * 128 : (b % blocks + 1) * 128] - z * cols
            line = jnp.where((line >= 0) & (line < cols), line, -chunks * CHUNK * 4).astype(jnp.float32)
            core = c if b < blocks else 1 - c
            out = pl.ds(pl.multiple_of(core * own_tokens + (b % blocks) * 128, 128), 128)
            id_cols[out, :] = jnp.transpose(jnp.broadcast_to(line, (128, 128)))

    def clear():
        m_acc[...] = jnp.full(m_acc.shape, LOW, jnp.float32)
        s_acc[...] = jnp.zeros(s_acc.shape, jnp.float32)
        q_acc[...] = jnp.zeros(q_acc.shape, jnp.float32)
        p_acc[...] = jnp.zeros(p_acc.shape, jnp.float32)

    w_pair.start()
    id_copy.start()

    @pl.loop(1, zs)
    def _(k):
        remote(gains.at[z], gains.at[z], send_sem.at[7], g_sem.at[k], line_peer(k)).start()

    ops, _ = plan(chunks // 2, subs)
    extra = {0: ref_start, 24: clear, 26: ids_to_columns, 60: ref_pick, 64: ref_send, 110: ref_wait}
    gains_here = False
    for number, op in enumerate(ops):
        if op[0] == "send":
            move(op[1], op[2]).start()
        elif op[0] == "wait":
            item = op[1]
            if item[0] == "p":
                ref = token_rows(1 - c, item[1])
                remote(ref, ref, send_sem.at[4], n_sem.at[item[1]], partner).wait_recv()
            elif item[0] == "w" and item[1:3] == (0, 0):
                w_pair.wait_recv()
            elif item[0] == "w":
                ref, sem = w_piece(*item[1:])
                remote(ref, ref, send_sem.at[2], sem, partner).wait_recv()
            elif item[1] != 0:
                ref, sem = h_piece(*item[1:])
                remote(ref, ref, send_sem.at[3], sem, partner).wait_recv()
        elif op[0] == "norm":
            if not gains_here:
                gains_here = True

                @pl.loop(1, zs)
                def _(k):
                    src = gains.at[(z + zs - k) % zs]
                    remote(src, src, send_sem.at[7], g_sem.at[k], partner).wait_recv()

            normalize(op[1])
            pair_tokens(op[1]).start()
        else:
            chunk(2 * op[1] + (1 - lo if op[2] else lo))
        if number in extra:
            extra[number]()

    stat_rows[...] = jnp.zeros(stat_rows.shape, jnp.float32)

    def reduce_block(b, _):
        rows = pl.ds(pl.multiple_of(b * 128, 128), 128)
        lane_max = m_acc[rows, :]
        top = jnp.max(lane_max, axis=1, keepdims=True)
        scale = jnp.exp(lane_max - top)
        total = jnp.sum(s_acc[rows, :] * scale, axis=1, keepdims=True)
        square = jnp.sum(q_acc[rows, :] * (scale * scale), axis=1, keepdims=True)
        chosen = jnp.sum(p_acc[rows, :], axis=1, keepdims=True)
        place = jnp.where(b // blocks == c, 0, 16) + b % blocks
        spread = stat_rows[...]
        for k, value in enumerate((top, total, square, chosen)):
            spread = jnp.where(lane == place + k * blocks, value, spread)
        stat_rows[...] = spread
        return 0

    lax.fori_loop(0, 2 * blocks, reduce_block, 0)
    turned = jnp.transpose(stat_rows[...])
    stat_rows[...] = turned
    give = remote(stat_rows.at[pl.ds(16, 16)], stat_peer, send_sem.at[8], pair_sem.at[2], partner)
    give.start()
    give.wait_recv()

    def merge(parts):
        top = functools.reduce(jnp.maximum, [p[0:4] for p in parts])
        total = square = chosen = 0.0
        for p in parts:
            scale = jnp.exp(p[0:4] - top)
            total += p[4:8] * scale
            square += p[8:12] * (scale * scale)
            chosen += p[12:16]
        return top, total, square, chosen

    stat_all[z] = jnp.concatenate(merge([stat_rows[0:16, :], stat_peer[...]]), axis=0)

    @pl.loop(1, zs)
    def _(k):
        remote(stat_all.at[z], stat_all.at[z], send_sem.at[9], s_sem.at[k], line_peer(k)).start()

    @pl.loop(1, zs)
    def _(k):
        src = stat_all.at[(z + zs - k) % zs]
        remote(src, src, send_sem.at[9], s_sem.at[k], partner).wait_recv()

    top, total, square, chosen = merge([stat_all[k] for k in range(zs)])
    new_logp = chosen - top - jnp.log(total)
    prob_square = square / (total * total)

    def lines(ref):
        return jnp.concatenate([ref[:, b * 128 : (b + 1) * 128] for b in range(blocks)], axis=0)

    old_logp, advantages = lines(old), lines(adv)
    ref_logp = jnp.concatenate(
        [jnp.where(lane < 64, ref_all[2 * b], ref_all[2 * b + 1]) for b in range(blocks)], axis=0
    )
    position = lax.broadcasted_iota(jnp.int32, (blocks, 128), 0) * 128 + lax.broadcasted_iota(
        jnp.int32, (blocks, 128), 1
    )
    live = jnp.where(position < lens[0], 1.0, 0.0)
    shift = new_logp - old_logp
    prob_ratio = jnp.exp(jnp.clip(shift, -log_limit, log_limit))
    clipped = jnp.clip(prob_ratio, 1.0 - clip_eps, 1.0 + clip_eps)
    plain_term = prob_ratio * advantages
    bounded_term = clipped * advantages
    surrogate = jnp.minimum(plain_term, bounded_term)
    ref_gap = ref_logp - new_logp
    gap_clip = jnp.clip(ref_gap, -log_limit, log_limit)
    gap_exp = jnp.exp(gap_clip)
    kl_term = gap_exp - gap_clip - 1.0
    token_loss = live * (kl_coef * kl_term - surrogate)
    inside_gap = jnp.where(jnp.abs(ref_gap) < log_limit, 1.0, 0.0)
    inside_ratio = jnp.where(jnp.abs(shift) < log_limit, 1.0, 0.0)
    active = jnp.where(plain_term <= bounded_term, 1.0, 0.0)
    grad = live * (kl_coef * (1.0 - gap_exp) * inside_gap - advantages * prob_ratio * active * inside_ratio)
    grad_square = grad * grad * (prob_square - 2.0 * jnp.exp(new_logp) + 1.0)

    def whole(array):
        return jnp.sum(jnp.sum(array, axis=0, keepdims=True), axis=1, keepdims=True)

    own_sums = jnp.zeros((1, 128), jnp.float32)
    for k, value in enumerate((live, token_loss, live * kl_term, grad_square)):
        own_sums = jnp.where(lane == k, whole(value), own_sums)
    tot_all[me] = own_sums

    @pl.loop(1, 32)
    def _(k):
        remote(tot_all.at[me], tot_all.at[me], send_sem.at[10], t_sem.at[k], plane_peer(k)).start()

    for b in range(blocks):
        logp_out[:, b * 128 : (b + 1) * 128] = new_logp[b : b + 1, :]
        loss_out[:, b * 128 : (b + 1) * 128] = token_loss[b : b + 1, :]

    @pl.loop(1, 32)
    def _(k):
        src = tot_all.at[(me + 32 - k) % 32]
        remote(src, src, send_sem.at[10], t_sem.at[k], partner).wait_recv()

    sums = functools.reduce(jnp.add, [tot_all[k] for k in range(32)])
    count, loss, kl, grads = [
        jnp.sum(jnp.where(lane == k, sums, 0.0), axis=1, keepdims=True) for k in range(4)
    ]
    sum_out[...] = jnp.where(
        lane == 0, loss / count, jnp.where(lane == 1, kl / count, jnp.sqrt(grads / count))
    )

    def left(src, k):
        remote(src, src, send_sem.at[k], local_sem.at[0], partner).wait_send()

    left(ids, 0)
    left(w_send, 1)
    left(w_all.at[:, 0 : 7 * 256, :], 2)
    left(hid.at[0 : zs - 1], 3)
    left(normed.at[0:own_tokens, :], 4)
    left(ref_rows.at[0:31], 5)
    left(ref_all.at[0 : zs - 1], 6)
    left(gains.at[0 : zs - 1], 7)
    left(stat_peer, 8)
    left(stat_all.at[0 : zs - 1], 9)
    left(tot_all.at[0:31], 10)


def shards(hidden, norm_gain, head_weight, token_ids, lengths, old_logp, advantages, rollout_logp, rollout_row):
    tokens, features = hidden.shape
    rows_dev, cols = head_weight.shape
    zs = lax.axis_size("tensor")
    depth = features * zs
    chunks = 8
    vmem = pl.BlockSpec(memory_space=pltpu.VMEM)
    smem = pl.BlockSpec(memory_space=pltpu.SMEM)
    anywhere = pl.BlockSpec(memory_space=pl.ANY)
    f32, bf16 = jnp.float32, jnp.bfloat16
    dma = pltpu.SemaphoreType.DMA
    new_logp, token_loss, summary = pl.pallas_call(
        kernel,
        out_shape=(
            jax.ShapeDtypeStruct((1, tokens), f32),
            jax.ShapeDtypeStruct((1, tokens), f32),
            jax.ShapeDtypeStruct((1, 128), f32),
        ),
        in_specs=[anywhere, vmem, anywhere, vmem, smem, vmem, vmem, vmem, smem],
        out_specs=(vmem, vmem, vmem),
        scratch_shapes=[
            pltpu.VMEM((chunks, depth, CHUNK), bf16),
            pltpu.VMEM((rows_dev, cols), bf16),
            pltpu.VMEM((chunks, rows_dev, CHUNK), bf16),
            pltpu.VMEM((zs, tokens, features), bf16),
            pltpu.VMEM((2 * tokens, depth), bf16),
            pltpu.VMEM((1, tokens), jnp.int32),
            pltpu.VMEM((2 * tokens, 128), f32),
            pltpu.VMEM((2 * tokens, 128), f32),
            pltpu.VMEM((2 * tokens, 128), f32),
            pltpu.VMEM((2 * tokens, 128), f32),
            pltpu.VMEM((2 * tokens, 128), f32),
            pltpu.VMEM((128, 128), f32),
            pltpu.VMEM((16, 128), f32),
            pltpu.VMEM((zs, 16, 128), f32),
            pltpu.VMEM((32, 1, 128), f32),
            pltpu.VMEM((zs, 1, 128), f32),
            pltpu.VMEM((zs, 1, features), f32),
            pltpu.VMEM((32, 1, 128), f32),
            dma((2,)),
            dma((8, chunks)),
            dma((zs, tokens // SUB)),
            dma((tokens // SUB,)),
            dma((zs,)),
            dma((32,)),
            dma((zs,)),
            dma((zs,)),
            dma((32,)),
            dma((3,)),
            dma((11,)),
        ],
        compiler_params=pltpu.CompilerParams(
            collective_id=0, has_side_effects=True, vmem_limit_bytes=48 * 1024 * 1024
        ),
    )(
        hidden, norm_gain.reshape(1, features), head_weight, token_ids, lengths, old_logp, advantages, rollout_logp,
        rollout_row,
    )
    return new_logp, token_loss, summary[0, :3]


def solution(mesh):
    in_specs = (
        P(("dp", "fsdp"), "tensor"),
        P("tensor"),
        P("fsdp", "tensor"),
        P(("dp", "fsdp"), None),
        P(("dp", "fsdp")),
        P(("dp", "fsdp"), None),
        P(("dp", "fsdp"), None),
        P(("dp", "fsdp"), "tensor"),
        P(("dp", "fsdp")),
    )
    out_specs = (P(("dp", "fsdp"), None), P(("dp", "fsdp"), None), P())
    return jax.shard_map(shards, mesh=mesh, in_specs=in_specs, out_specs=out_specs, check_vma=False)
```

time: 219 us -> 84.7 us (0.39)
  waiting for transfers between devices: 113 us -> 0 us
  Pallas kernels: 0 us -> 79.3 us
  starting transfers between devices: 36 us -> 0 us
  between operations: 19.3 us -> 2.06 us
  matrix products: 14.8 us -> 0 us
  other arithmetic: 14.5 us -> 0 us
  blocking collectives: 13.1 us -> 0 us
  local copies, waits for them, and re-layouts: 8.21 us -> 3.28 us
    pallas_call x0 -> x1, Pallas kernels: none -> 79.3 us  [shards(): pl.pallas_call(kernel, out_shape=(jax.ShapeDtypeStruct((1, tokens), f32),...]
    all_to_all x6 -> x0, waiting for transfers between devices: 69 us -> none  [copy_for_each(): return lax.all_to_all(copies, axis, split_axis=0, concat_axis=0, tiled=True)]
    all_gather x1 -> x0, waiting for transfers between devices: 43.2 us -> none  [shards(): lax.all_gather(head_weight, 'fsdp', axis=0, tiled=True)]
    all_to_all x6 -> x0, starting transfers between devices: 35.9 us -> none  [copy_for_each(): return lax.all_to_all(copies, axis, split_axis=0, concat_axis=0, tiled=True)]
    dot_general x1 -> x0, matrix products: 14.8 us -> none  [shards(): jnp.dot(normed, lax.all_gather(head_weight, 'fsdp', axis=0, tiled=True),...]
    all_to_all x1 -> x0, blocking collectives: 13.1 us -> none  [copy_for_each(): return lax.all_to_all(copies, axis, split_axis=0, concat_axis=0, tiled=True)]
    reduce_sum x6 -> x0, other arithmetic: 7.95 us -> none  [the longest x1 5.43 us: exp_sums(): return (jnp.sum(shifted, axis=1), jnp.sum(shifted * shifted, axis=1))]
    broadcast_in_dim x8 -> x0, local copies, waits for them, and re-layouts: 5.14 us -> none  [copy_for_each(): copies = jnp.broadcast_to(array, (lax.axis_size(axis), *array.shape))]
  transfers between devices with their start and end apart: 7 -> 0, of which waited for: 6 -> 0; matrix products, arithmetic and copies ran while one was open for 14% -> 0% of each run, Pallas kernels for 0% -> 0%
where the time goes in v1:
time: 84.7 us; the launch traced here: 84.6 us
  Pallas kernels  79.3 us (94%)
  local copies, waits for them, and re-layouts  3.28 us (4%)
  between operations  2.06 us (2%)
    pallas_call x1, Pallas kernels, shards(): pl.pallas_call(kernel, out_shape=(jax.ShapeDtypeStruct((1, tokens), f32),...  79.3 us
    unnamed x15, local copies, waits for them, and re-layouts  2.76 us

profile of v1, /device:TPU:1, one launch (start us, length us, event | category | flops | bytes accessed | tf_op | source)
XLA Modules:
  0.0 84.6 jit_solution(14788635745665335021)
XLA Ops:
  1.3 0.0 copy-start.5
  1.9 0.0 copy-done.5
  2.0 0.0 copy-start
  2.0 0.0 copy-start.1
  2.0 0.0 copy-start.2
  2.0 0.0 copy-start.3
  2.0 0.0 copy-start.4
  2.0 1.6 %copy.12.weight = bf16[128,4016]{1,0:T(8,128)(2,1)S(1)} copy(bf16[128,4016]{0,1:T(8,128)(2,1)} %param.11) | data formatting | bytes 2056192 | tf_op args[2]
  3.6 0.0 copy-done
  3.6 0.0 copy-done.1
  3.6 0.0 copy-done.2
  3.6 0.0 copy-done.3
  3.6 0.0 copy-done.4
  3.7 79.3 %shard_map.112 = (f32[1,512]{1,0:T(1,128)S(1)}, f32[1,512]{1,0:T(1,128)S(1)}, f32[1,128]{1,0:T(1,128)S(1)}) custom-call(bf16[512,256]{1,0:T(8,128)(2,1)S(1)} %copy-done, bf16[1,256]{1,0:T(2,128)(2,1)S(1)} %reshape.9.gain, bf16[128,4016]{1,0:T(8,128)(2,1)S(1)} %copy.12.weight, s32[1,512]{1,0:T(1,128)S(1)} %copy-done.1, s32[1]{0:T(128)S(6)} %copy.15.lens, ...), custom_call_target="tpu_custom_call" | custom-call | tf_op jit(solution)/shard_map/pallas_call | solution.py:509
  82.9 0.5 slice_bitcast_fusion
  83.4 0.6 copy.17
  84.0 0.6 copy.18
  (1 shorter events, 0.0 us)
Async XLA Ops:
  1.3 0.7 copy-start.5
  2.0 1.6 %copy-start = (bf16[512,256]{1,0:T(8,128)(2,1)S(1)}, bf16[512,256]{1,0:T(8,128)(2,1)}, u32[]{:S(2)}) copy-start(bf16[512,256]{1,0:T(8,128)(2,1)} %hidden.1) | copy-start | bytes 786436
  2.0 1.6 %copy-start.1 = (s32[1,512]{1,0:T(1,128)S(1)}, s32[1,512]{1,0:T(1,128)}, u32[]{:S(2)}) copy-start(s32[1,512]{1,0:T(1,128)} %ids.1) | copy-start | bytes 6148
  2.0 1.6 %copy-start.2 = (f32[1,512]{1,0:T(1,128)S(1)}, f32[1,512]{1,0:T(1,128)}, u32[]{:S(2)}) copy-start(f32[1,512]{1,0:T(1,128)} %old.1) | copy-start | bytes 6148
  2.0 1.6 %copy-start.3 = (f32[1,512]{1,0:T(1,128)S(1)}, f32[1,512]{1,0:T(1,128)}, u32[]{:S(2)}) copy-start(f32[1,512]{1,0:T(1,128)} %adv.1) | copy-start | bytes 6148
  2.0 1.6 %copy-start.4 = (f32[1,64]{1,0:T(1,128)S(1)}, f32[1,64]{1,0:T(1,128)}, u32[]{:S(2)}) copy-start(f32[1,64]{1,0:T(1,128)} %roll.1) | copy-start | bytes 772

commit v2 on v0

v2 whole, which is shorter than its diff:
```python
import collections
import functools
import heapq

import jax
import jax.numpy as jnp
from jax import lax
from jax.experimental import pallas as pl
from jax.experimental.pallas import tpu as pltpu
from jax.sharding import PartitionSpec as P

clip_eps = 0.2
kl_coef = 0.2
log_limit = 10.0
norm_eps = 1e-06

MESH = pl.DeviceIdType.MESH
LOW = -1e30
CHUNK = 256
SUB = 128
DEPTH = 2
BATCH = 4
CHUNKS = 4
SUBS = 4
NEAR = (0, 1, 3, 6, 7)
TUNE = dict(y_far=-0.23, y_col=0.99, h_dy=(14.71, 7.92, -16.21, 18.43), z_hop=-74.15, z_sub=-20.38, z_late=-48.75, l_hop=-29.58, l_sub=22.48, by_h=())


def way_in(item):
    if item[0] == "w":
        _, col, dy, j = item
        if col == 0:
            if dy == 2:
                return "yp" if j < CHUNKS // 2 else "ym"
            return {0: None, 3: "yp", 1: "ym"}[dy]
        if dy in (0, 2) or j in TUNE["by_h"]:
            return "h"
        return "yp" if dy == 3 else "ym"
    _, who, dz, sub = item
    if who == 0 and dz == 0:
        return None
    if who == 1 and dz in NEAR:
        return "l"
    if dz == 4:
        return "zp" if sub < SUBS // 2 else "zm"
    return "zp" if dz > 4 else "zm"


def arrives_as(link, item):
    if item[0] == "w":
        _, col, dy, j = item
        if link == "h":
            return ("w", 1 - col, dy, j)
        return ("w", col, (dy + (3 if link == "yp" else 1)) % 4, j)
    _, who, dz, sub = item
    if link == "l":
        return ("h", 1 - who, dz, sub)
    return ("h", who, (dz + (7 if link == "zp" else 1)) % 8, sub)


def links_of(item):
    names = ("yp", "ym", "h") if item[0] == "w" else ("zp", "zm", "l")
    return [n for n in names if way_in(arrives_as(n, item)) == n]


def rank(link, item):
    t = TUNE
    if item[0] == "w":
        _, col, dy, j = item
        if link == "h":
            return (j + t["h_dy"][dy], dy)
        return (j + (t["y_far"] if dy else 0.0) + t["y_col"] * col, dy)
    _, who, dz, sub = item
    hops = min(dz, 8 - dz)
    if link == "l":
        return (hops * t["l_hop"] + sub * t["l_sub"], dz)
    return (hops * t["z_hop"] + sub * t["z_sub"] + who * t["z_late"], dz)


def plan():
    wire = {"w": 2.85, "h": 1.43}
    delay = 2.0
    norm_time, jobs_time, unit_time = 0.45, 0.15, 0.4
    names = ("zp", "zm", "l", "yp", "ym", "h")
    free = dict.fromkeys(names, 0.0)
    ends = {n: [] for n in names}
    ready = {n: [] for n in names}
    arrivals, ops = [], []
    for sub in range(SUBS):
        heapq.heappush(arrivals, (0.0, ("h", 0, 0, sub)))
    for j in range(CHUNKS):
        heapq.heappush(arrivals, (1.0 + 0.2 * j, ("w", 0, 0, j)))
    tokens = [(who, sub) for sub in range(SUBS) for who in (0, 1)]
    missing = {("c", j): 8 for j in range(CHUNKS)}
    missing.update({("n", *w): 8 for w in tokens})
    token_parts = {w: 2 for w in tokens}
    norms, units, chunks_here, tokens_here = [], [], [], []
    now = 0.0

    def top_up():
        for n in names:
            ends[n] = [e for e in ends[n] if e > now]
            while ready[n] and len(ends[n]) < DEPTH:
                _, item = heapq.heappop(ready[n])
                end = max(now, free[n]) + wire[item[0]]
                free[n] = end
                ends[n].append(end)
                ops.append(("send", n, item))
                heapq.heappush(arrivals, (end + delay, arrives_as(n, item)))

    def part_of(w):
        token_parts[w] -= 1
        if token_parts[w] == 0:
            tokens_here.append(w)
            units.extend((*w, j) for j in chunks_here)

    while arrivals or norms or units:
        if arrivals and arrivals[0][0] <= now:
            _, item = heapq.heappop(arrivals)
            ops.append(("wait", item))
            if item[0] == "p":
                part_of(item[1:])
                continue
            for n in links_of(item):
                heapq.heappush(ready[n], (rank(n, item), item))
            if not arrivals or arrivals[0][0] > now:
                top_up()
            key = ("c", item[3]) if item[0] == "w" else ("n", item[1], item[3])
            missing[key] -= 1
            if missing[key] == 0:
                if key[0] == "c":
                    chunks_here.append(key[1])
                    units.extend((*w, key[1]) for w in tokens_here)
                else:
                    norms.append(key[1:])
        elif norms:
            who_sub = norms.pop(0)
            now += norm_time
            ops.append(("norm", who_sub))
            heapq.heappush(arrivals, (now + 1.8, ("p", *who_sub)))
            part_of(who_sub)
            top_up()
        elif units:
            batch = sorted(units[:BATCH])
            del units[:BATCH]
            now += jobs_time + unit_time * len(batch)
            ops.append(("jobs", tuple(batch)))
            top_up()
        else:
            now = arrivals[0][0]
            top_up()
    return ops, now


def kernel(
    hidden, gain_in, weight, ids_in, lens, old_in, adv_in, roll_in, row,
    logp_out, loss_out, sum_out,
    w_all, hid, normed, ids, id_row, m_acc, s_acc, q_acc, p_acc,
    stat_rows, stat_quad, stat_all, ref_rows, ref_all, gains, tot_all, gain, old, adv, roll,
    local_sem, own_sem, wp_sem, w_sem, h_sem, n_sem, g_sem, all_sem, send_sem,
):
    lo, f, z = lax.axis_index("dp"), lax.axis_index("fsdp"), lax.axis_index("tensor")
    hi, y, c = f // 8, (f // 2) % 4, f % 2
    me = lo * 16 + f
    side = (lo + hi) % 2
    quarter = 2 * side + c
    cols, rows_dev = weight.shape
    zs, features = stat_all.shape[0], hid.shape[2]
    blocks = ids_in.shape[1] // 128
    last = cols - (4 * CHUNKS - 1) * CHUNK
    group = hi * 4 + y

    def at(hi_, lo_, y_, c_, z_):
        return {"dp": lo_, "fsdp": hi_ * 8 + y_ * 2 + c_, "tensor": z_}

    quad = [None, at(hi, lo, y, 1 - c, z), at(hi, 1 - lo, y, c, z), at(hi, 1 - lo, y, 1 - c, z)]
    partner = quad[1]
    target = {
        "yp": at(hi, lo, (y + 1) % 4, c, z),
        "ym": at(hi, lo, (y + 3) % 4, c, z),
        "h": at(1 - hi, 1 - lo, y, c, z),
        "l": quad[2],
        "zp": at(hi, lo, y, c, (z + 1) % zs),
        "zm": at(hi, lo, y, c, (z + zs - 1) % zs),
    }

    def plane_peer(k):
        other = (me + k) % 32
        return {"dp": other // 16, "fsdp": other % 16, "tensor": z}

    def line_peer(k):
        return {"dp": lo, "fsdp": f, "tensor": (z + k) % zs}

    def remote(src, dst, s, r, device):
        return pltpu.make_async_remote_copy(
            src_ref=src, dst_ref=dst, send_sem=s, recv_sem=r, device_id=device, device_id_type=MESH
        )

    def received(dst, r):
        remote(dst, dst, send_sem.at[0], r, partner).wait_recv()

    barrier = pltpu.get_barrier_semaphore()
    for device in (*quad[1:], *(target[n] for n in ("yp", "ym", "h", "zp", "zm"))):
        pl.semaphore_signal(barrier, inc=1, device_id=device, device_id_type=MESH)

    lane0 = pl.multiple_of(group * 256 + c * rows_dev, 128)

    def sized(j, owner, act):
        if j < CHUNKS - 1:
            act(CHUNK)
            return

        @pl.when(owner < 3)
        def _():
            act(CHUNK)

        @pl.when(owner == 3)
        def _():
            act(last)

    def own_weights(j, count):
        src = weight.at[pl.ds(pl.multiple_of((quarter * CHUNKS + j) * CHUNK, CHUNK), count), :]
        return pltpu.make_async_copy(src, w_all.at[j, pl.ds(0, count), pl.ds(lane0, 128)], own_sem.at[j])

    def pair_weights(j, count, owner):
        src = weight.at[pl.ds(pl.multiple_of((owner * CHUNKS + j) * CHUNK, CHUNK), count), :]
        dst = w_all.at[j, pl.ds(0, count), pl.ds(lane0, 128)]
        return remote(src, dst, send_sem.at[12 if j < CHUNKS - 1 else 0], wp_sem.at[j], partner)

    small = [
        pltpu.make_async_copy(src, dst, local_sem.at[k])
        for k, (src, dst) in enumerate(
            ((gain_in, gain), (roll_in, roll), (ids_in, ids.at[0]), (old_in, old), (adv_in, adv))
        )
    ]
    hid_in = pltpu.make_async_copy(hidden, hid.at[z], local_sem.at[5])
    hid_in.start()
    small[0].start()
    small[2].start()
    for j in range(CHUNKS):
        sized(j, quarter, lambda n, j=j: own_weights(j, n).start())
    for k in (1, 3, 4):
        small[k].start()

    @pl.when(quarter == 3)
    def _():
        pad = jnp.zeros((CHUNK - last, 256), jnp.bfloat16)
        w_all[CHUNKS - 1, last:CHUNK, pl.ds(pl.multiple_of(group * 256, 256), 256)] = pad

    lane = lax.broadcasted_iota(jnp.int32, (1, 128), 1)
    m_acc[...] = jnp.full(m_acc.shape, LOW, jnp.float32)
    s_acc[...] = jnp.zeros(s_acc.shape, jnp.float32)
    q_acc[...] = jnp.zeros(q_acc.shape, jnp.float32)
    p_acc[...] = jnp.zeros(p_acc.shape, jnp.float32)
    small[0].wait()
    gains[z] = gain[...].astype(jnp.float32).reshape(1, features)
    small[1].wait()
    ref_rows[0] = jnp.concatenate([roll[...], roll[...]], axis=1)
    small[2].wait()
    pl.semaphore_wait(barrier, 8)

    ops = plan()[0]
    first_who, first_sub = next(op[1] for op in ops if op[0] == "norm")
    assert first_who == 0

    def w_piece(col, dy, j):
        g = (1 - hi if col else hi) * 4 + (y + dy) % 4
        return w_all.at[j, :, pl.ds(pl.multiple_of(g * 256, 256), 256)], w_sem.at[g, j]

    def h_piece(who, dz, sub):
        owner = who * zs + (z + dz) % zs
        return hid.at[owner, pl.ds(sub * SUB, SUB), :], h_sem.at[owner, sub]

    def with_gain(link, item):
        return link[0] == "z" and item[1] == 0 and item[3] == first_sub

    def send(link, item):
        if item[0] == "w":
            ref, sem = w_piece(*item[1:])
            remote(ref, ref, send_sem.at[1], sem, target[link]).start()
            return
        ref, sem = h_piece(*item[1:])
        other = h_piece(1 - item[1], *item[2:]) if link == "l" else (ref, sem)
        remote(ref, other[0], send_sem.at[2 if link == "l" else 3], other[1], target[link]).start()
        if with_gain(link, item):
            k = (z + item[2]) % zs
            remote(gains.at[k], gains.at[k], send_sem.at[4], g_sem.at[k], target[link]).start()

    def place(who, sub, core):
        return pl.multiple_of(((who * SUBS + sub) * 2 + core) * SUB, SUB)

    def wait(item):
        if item[0] == "p":
            received(normed.at[pl.ds(place(*item[1:], 1 - c), SUB), :], n_sem.at[item[1], item[2]])
        elif item[0] == "w" and item[1:3] == (0, 0):
            j = item[3]
            sized(j, quarter, lambda n: own_weights(j, n).wait())
            sized(j, quarter, lambda n: received(w_all.at[j, pl.ds(0, n), pl.ds(lane0, 128)], wp_sem.at[j]))
        elif item[0] == "w":
            received(*w_piece(*item[1:]))
        elif item[1:3] != (0, 0):
            received(*h_piece(*item[1:]))
            if item[1] == 0 and item[3] == first_sub:
                k = (z + item[2]) % zs
                received(gains.at[k], g_sem.at[k])

    def normalize(who, sub):
        gain_rows = [gains[k] for k in range(zs)]
        for t in range(0, SUB, 32):
            rows = slice(sub * SUB + t, sub * SUB + t + 32)
            squares = jnp.zeros((32, features), jnp.float32)
            for k in range(zs):
                part = hid[who * zs + k, rows, :].astype(jnp.float32)
                squares += part * part
            mean = jnp.sum(squares, axis=1, keepdims=True) * (1.0 / (zs * features))
            inv = lax.rsqrt(mean + norm_eps)
            out = pl.ds(pl.multiple_of(place(who, sub, c) + t, 32), 32)
            for k in range(zs):
                part = hid[who * zs + k, rows, :].astype(jnp.float32)
                normed[out, k * features : (k + 1) * features] = (part * inv * gain_rows[k]).astype(jnp.bfloat16)

        ref = normed.at[pl.ds(place(who, sub, c), SUB), :]
        remote(ref, ref, send_sem.at[5], n_sem.at[who, sub], partner).start()

    def job(who, sub, j):
        base = (quarter * CHUNKS + j) * CHUNK
        start = (who * SUBS + sub) * 2 * SUB
        tokens = slice(start, start + 2 * SUB)
        logits = lax.dot_general(
            w_all[j], normed[tokens, :], (((1,), (1,)), ((), ())), preferred_element_type=jnp.float32
        ).reshape(CHUNK // 8, 8, 2 * SUB)
        shape = (CHUNK // 8, 8, 1)
        column = lax.broadcasted_iota(jnp.int32, shape, 0) * 8 + lax.broadcasted_iota(jnp.int32, shape, 1)
        if j == CHUNKS - 1:
            logits = jnp.where(column < cols - base, logits, LOW)
        wanted = (id_row[:, tokens] - base)[None]
        p_acc[:, tokens] += jnp.sum(jnp.where(column == wanted, logits, 0.0), axis=0)
        old_max = m_acc[:, tokens]
        new_max = jnp.maximum(old_max, jnp.max(logits, axis=0))
        scale = jnp.exp(old_max - new_max)
        exps = jnp.exp(logits - new_max[None])
        s_acc[:, tokens] = s_acc[:, tokens] * scale + jnp.sum(exps, axis=0)
        q_acc[:, tokens] = q_acc[:, tokens] * (scale * scale) + jnp.sum(exps * exps, axis=0)
        m_acc[:, tokens] = new_max

    def ids_to_row():
        received(ids.at[1:4], all_sem.at[0])
        for s in range(4):
            for sub in range(SUBS):
                line = ids[s, :, sub * 128 : (sub + 1) * 128] - z * cols
                line = jnp.where((line >= 0) & (line < cols), line, -(1 << 20))
                id_row[:, pl.ds(place(s // 2, sub, (c + s) % 2), 128)] = line

    def to_plane(array, s, r):
        @pl.loop(0, 31)
        def _(i):
            k = (i + 15) % 31 + 1
            remote(array.at[0], array.at[k], send_sem.at[s], all_sem.at[r], plane_peer(k)).start()

    def to_line(array, s, r):
        for k in (4, 3, 5, 2, 6, 1, 7):
            remote(array.at[0], array.at[k], send_sem.at[s], all_sem.at[r], line_peer(k)).start()

    def all_received(array, r):
        received(array.at[1:], all_sem.at[r])

    def ref_start():
        to_plane(ref_rows, 6, 1)

    def ref_pick():
        all_received(ref_rows, 1)
        ref_all[0] = ref_rows[(me + 32 - row[0]) % 32]

    def ref_send():
        to_line(ref_all, 7, 2)

    def ref_wait():
        all_received(ref_all, 2)

    other = 2 * side + 1 - c
    for j in range(CHUNKS):
        sized(j, other, lambda n, j=j: pair_weights(j, n, other).start())
    for s in range(1, 4):
        remote(ids.at[0], ids.at[s], send_sem.at[8], all_sem.at[0], quad[s]).start()
    hid_in.wait()

    batches = 0
    extra = {1: ref_start, 4: ref_pick, 5: ref_send, 8: ref_wait}
    for number, op in enumerate(ops):
        if op[0] == "send":
            send(op[1], op[2])
        elif op[0] == "wait":
            wait(op[1])
        elif op[0] == "norm":
            normalize(*op[1])
        else:
            for unit in op[1]:
                job(*unit)
            batches += 1
            if batches in extra:
                extra[batches]()
        if number == 40:
            ids_to_row()

    top = jnp.max(m_acc[...], axis=0, keepdims=True)
    scale = jnp.exp(m_acc[...] - top)
    total = jnp.sum(s_acc[...] * scale, axis=0, keepdims=True)
    square = jnp.sum(q_acc[...] * (scale * scale), axis=0, keepdims=True)
    chosen = jnp.sum(p_acc[...], axis=0, keepdims=True)
    for who in (0, 1):
        for core in (0, 1):
            starts = [((who * SUBS + sub) * 2 + core) * SUB for sub in range(SUBS)]
            stat_rows[who * 2 + (core + c) % 2] = jnp.concatenate(
                [value[:, i : i + SUB] for value in (top, total, square, chosen) for i in starts], axis=0
            )
    for s in range(1, 4):
        remote(stat_rows.at[s], stat_quad.at[s - 1], send_sem.at[9], all_sem.at[3], quad[s]).start()
    received(stat_quad, all_sem.at[3])

    def merge(parts):
        top = functools.reduce(jnp.maximum, [p[0:4] for p in parts])
        total = square = chosen = 0.0
        for p in parts:
            scale = jnp.exp(p[0:4] - top)
            total += p[4:8] * scale
            square += p[8:12] * (scale * scale)
            chosen += p[12:16]
        return top, total, square, chosen

    stat_all[0] = jnp.concatenate(merge([stat_rows[0], *(stat_quad[s] for s in range(3))]), axis=0)

    to_line(stat_all, 10, 4)
    small[3].wait()
    small[4].wait()
    all_received(stat_all, 4)

    top, total, square, chosen = merge([stat_all[k] for k in range(zs)])
    new_logp = chosen - top - jnp.log(total)
    prob_square = square / (total * total)

    def lines(ref):
        return jnp.concatenate([ref[:, b * 128 : (b + 1) * 128] for b in range(blocks)], axis=0)

    old_logp, advantages = lines(old), lines(adv)
    ref_logp = jnp.concatenate(
        [jnp.where(lane < 64, ref_all[(z + zs - 2 * b) % zs], ref_all[(z + zs - 2 * b - 1) % zs]) for b in range(blocks)], axis=0
    )
    position = lax.broadcasted_iota(jnp.int32, (blocks, 128), 0) * 128 + lax.broadcasted_iota(
        jnp.int32, (blocks, 128), 1
    )
    live = jnp.where(position < lens[0], 1.0, 0.0)
    shift = new_logp - old_logp
    prob_ratio = jnp.exp(jnp.clip(shift, -log_limit, log_limit))
    clipped = jnp.clip(prob_ratio, 1.0 - clip_eps, 1.0 + clip_eps)
    plain_term = prob_ratio * advantages
    bounded_term = clipped * advantages
    surrogate = jnp.minimum(plain_term, bounded_term)
    ref_gap = ref_logp - new_logp
    gap_clip = jnp.clip(ref_gap, -log_limit, log_limit)
    gap_exp = jnp.exp(gap_clip)
    kl_term = gap_exp - gap_clip - 1.0
    token_loss = live * (kl_coef * kl_term - surrogate)
    inside_gap = jnp.where(jnp.abs(ref_gap) < log_limit, 1.0, 0.0)
    inside_ratio = jnp.where(jnp.abs(shift) < log_limit, 1.0, 0.0)
    active = jnp.where(plain_term <= bounded_term, 1.0, 0.0)
    grad = live * (kl_coef * (1.0 - gap_exp) * inside_gap - advantages * prob_ratio * active * inside_ratio)
    grad_square = grad * grad * (prob_square - 2.0 * jnp.exp(new_logp) + 1.0)

    def whole(array):
        return jnp.sum(jnp.sum(array, axis=0, keepdims=True), axis=1, keepdims=True)

    own_sums = jnp.zeros((1, 128), jnp.float32)
    for k, value in enumerate((live, token_loss, live * kl_term, grad_square)):
        own_sums = jnp.where(lane == k, whole(value), own_sums)
    tot_all[0] = own_sums

    to_plane(tot_all, 11, 5)

    for b in range(blocks):
        logp_out[:, b * 128 : (b + 1) * 128] = new_logp[b : b + 1, :]
        loss_out[:, b * 128 : (b + 1) * 128] = token_loss[b : b + 1, :]

    def left(src, sem):
        remote(src, src, sem, local_sem.at[0], partner).wait_send()

    left(weight.at[pl.ds(0, (CHUNKS - 1) * CHUNK), :], send_sem.at[12])
    sized(CHUNKS - 1, other, lambda n: left(weight.at[pl.ds(0, n), :], send_sem.at[0]))
    count = collections.Counter(
        op[1] if op[1] in ("l", "zp", "zm") else "w" for op in ops if op[0] == "send"
    )
    count["g"] = sum(op[0] == "send" and with_gain(op[1], op[2]) for op in ops)
    left(w_all.at[:, :, 0 : count["w"] // CHUNKS * 256], send_sem.at[1])
    left(hid.at[0 : count["l"] // SUBS], send_sem.at[2])
    left(hid.at[0 : (count["zp"] + count["zm"]) // SUBS], send_sem.at[3])
    left(gains.at[0 : count["g"]], send_sem.at[4])
    left(normed.at[0 : 2 * SUBS * SUB, :], send_sem.at[5])
    left(ref_rows.at[0:31], send_sem.at[6])
    left(ref_all.at[0 : zs - 1], send_sem.at[7])
    left(ids.at[1:4], send_sem.at[8])
    left(stat_quad, send_sem.at[9])
    left(stat_all.at[0 : zs - 1], send_sem.at[10])

    all_received(tot_all, 5)

    sums = functools.reduce(jnp.add, [tot_all[k] for k in range(32)])
    live_count, loss, kl, grads = [
        jnp.sum(jnp.where(lane == k, sums, 0.0), axis=1, keepdims=True) for k in range(4)
    ]
    sum_out[...] = jnp.where(
        lane == 0, loss / live_count, jnp.where(lane == 1, kl / live_count, jnp.sqrt(grads / live_count))
    )
    left(tot_all.at[0:31], send_sem.at[11])


def shards(hidden, norm_gain, head_weight, token_ids, lengths, old_logp, advantages, rollout_logp, rollout_row):
    tokens, features = hidden.shape
    rows_dev, cols = head_weight.shape
    zs = lax.axis_size("tensor")
    depth = features * zs
    vmem = pl.BlockSpec(memory_space=pltpu.VMEM)
    smem = pl.BlockSpec(memory_space=pltpu.SMEM)
    hbm = pl.BlockSpec(memory_space=pltpu.HBM)
    f32, bf16, i32 = jnp.float32, jnp.bfloat16, jnp.int32
    dma = pltpu.SemaphoreType.DMA
    new_logp, token_loss, summary = pl.pallas_call(
        kernel,
        out_shape=(
            jax.ShapeDtypeStruct((1, tokens), f32),
            jax.ShapeDtypeStruct((1, tokens), f32),
            jax.ShapeDtypeStruct((1, 128), f32),
        ),
        in_specs=[hbm, hbm, hbm, hbm, smem, hbm, hbm, hbm, smem],
        out_specs=(vmem, vmem, vmem),
        scratch_shapes=[
            pltpu.VMEM((CHUNKS, CHUNK, depth), bf16),
            pltpu.VMEM((2 * zs, tokens, features), bf16),
            pltpu.VMEM((4 * tokens, depth), bf16),
            pltpu.VMEM((4, 1, tokens), i32),
            pltpu.VMEM((1, 4 * tokens), i32),
            *[pltpu.VMEM((8, 4 * tokens), f32)] * 4,
            pltpu.VMEM((4, 16, 128), f32),
            pltpu.VMEM((3, 16, 128), f32),
            pltpu.VMEM((zs, 16, 128), f32),
            pltpu.VMEM((32, 1, 128), f32),
            pltpu.VMEM((zs, 1, 128), f32),
            pltpu.VMEM((zs, 1, features), f32),
            pltpu.VMEM((32, 1, 128), f32),
            pltpu.VMEM((features,), bf16),
            pltpu.VMEM((1, tokens), f32),
            pltpu.VMEM((1, tokens), f32),
            pltpu.VMEM((1, rollout_logp.shape[1]), f32),
            dma((6,)),
            dma((CHUNKS,)),
            dma((CHUNKS,)),
            dma((8, CHUNKS)),
            dma((2 * zs, SUBS)),
            dma((2, SUBS)),
            dma((zs,)),
            dma((6,)),
            dma((13,)),
        ],
        compiler_params=pltpu.CompilerParams(
            collective_id=0, has_side_effects=True, vmem_limit_bytes=64 * 1024 * 1024 - 256 * 1024
        ),
    )(
        hidden, norm_gain, head_weight.T, token_ids, lengths, old_logp, advantages, rollout_logp, rollout_row
    )
    return new_logp, token_loss, summary[0, :3]


def solution(mesh):
    in_specs = (
        P(("dp", "fsdp"), "tensor"),
        P("tensor"),
        P("fsdp", "tensor"),
        P(("dp", "fsdp"), None),
        P(("dp", "fsdp")),
        P(("dp", "fsdp"), None),
        P(("dp", "fsdp"), None),
        P(("dp", "fsdp"), "tensor"),
        P(("dp", "fsdp")),
    )
    out_specs = (P(("dp", "fsdp"), None), P(("dp", "fsdp"), None), P())
    return jax.shard_map(shards, mesh=mesh, in_specs=in_specs, out_specs=out_specs, check_vma=False)
```

time: 219 us -> 72 us (0.33)
  waiting for transfers between devices: 113 us -> 0 us
  Pallas kernels: 0 us -> 67.6 us
  starting transfers between devices: 36 us -> 0 us
  between operations: 19.3 us -> 1.95 us
  matrix products: 14.8 us -> 0 us
  other arithmetic: 14.5 us -> 0 us
  blocking collectives: 13.1 us -> 0 us
  local copies, waits for them, and re-layouts: 8.21 us -> 2.34 us
    all_to_all x6 -> x0, waiting for transfers between devices: 69 us -> none  [copy_for_each(): return lax.all_to_all(copies, axis, split_axis=0, concat_axis=0, tiled=True)]
    pallas_call x0 -> x1, Pallas kernels: none -> 67.6 us  [shards(): pl.pallas_call(kernel, out_shape=(jax.ShapeDtypeStruct((1, tokens), f32),...]
    all_gather x1 -> x0, waiting for transfers between devices: 43.2 us -> none  [shards(): lax.all_gather(head_weight, 'fsdp', axis=0, tiled=True)]
    all_to_all x6 -> x0, starting transfers between devices: 35.9 us -> none  [copy_for_each(): return lax.all_to_all(copies, axis, split_axis=0, concat_axis=0, tiled=True)]
    dot_general x1 -> x0, matrix products: 14.8 us -> none  [shards(): jnp.dot(normed, lax.all_gather(head_weight, 'fsdp', axis=0, tiled=True),...]
    all_to_all x1 -> x0, blocking collectives: 13.1 us -> none  [copy_for_each(): return lax.all_to_all(copies, axis, split_axis=0, concat_axis=0, tiled=True)]
    reduce_sum x6 -> x0, other arithmetic: 7.95 us -> none  [the longest x1 5.43 us: exp_sums(): return (jnp.sum(shifted, axis=1), jnp.sum(shifted * shifted, axis=1))]
    broadcast_in_dim x8 -> x0, local copies, waits for them, and re-layouts: 5.14 us -> none  [copy_for_each(): copies = jnp.broadcast_to(array, (lax.axis_size(axis), *array.shape))]
  transfers between devices with their start and end apart: 7 -> 0, of which waited for: 6 -> 0; matrix products, arithmetic and copies ran while one was open for 14% -> 0% of each run, Pallas kernels for 0% -> 0%
where the time goes in v2:
time: 72 us; the launch traced here: 71.9 us
  Pallas kernels  67.6 us (94%)
  local copies, waits for them, and re-layouts  2.34 us (3%)
  between operations  1.95 us (3%)
    pallas_call x1, Pallas kernels, shards(): pl.pallas_call(kernel, out_shape=(jax.ShapeDtypeStruct((1, tokens), f32),...  67.6 us
    unnamed x8, local copies, waits for them, and re-layouts  1.83 us

profile of v2, /device:TPU:1, one launch (start us, length us, event | category | flops | bytes accessed | tf_op | source)
XLA Modules:
  0.0 71.9 jit_solution(5178953595849300794)
XLA Ops:
  1.9 67.6 %shard_map.112 = (f32[1,512]{1,0:T(1,128)}, f32[1,512]{1,0:T(1,128)}, f32[1,128]{1,0:T(1,128)}) custom-call(bf16[512,256]{1,0:T(8,128)(2,1)} %hidden.1, bf16[256]{0:T(256)(128)(2,1)} %gain_in.1, bf16[4016,128]{1,0:T(8,128)(2,1)} %bitcast.3, s32[1,512]{1,0:T(1,128)} %ids_in.1, s32[1]{0:T(128)S(6)} %copy.14.lens, f32[1,512]{1,0:T(1,128)} %old_in.1, ...), custom_call_target="tpu_custom_call" | custom-call | tf_op jit(solution)/shard_map/pallas_call | solution.py:525
  69.5 0.0 copy-start.2
  69.5 0.0 copy-start.1
  69.5 0.6 copy-done.2
  70.1 0.5 slice_bitcast_fusion
  70.6 0.0 copy-done.1
  70.6 0.0 copy-start
  70.6 0.6 copy.16
  71.2 0.1 copy-done
  71.3 0.6 copy.17
Async XLA Ops:
  69.5 0.6 copy-start.2
  69.5 1.1 %copy-start.1 = (f32[1,512]{1,0:T(1,128)S(1)}, f32[1,512]{1,0:T(1,128)}, u32[]{:S(2)}) copy-start(f32[1,512]{1,0:T(1,128)} %get-tuple-element.12) | copy-start | bytes 6148
  70.6 0.7 copy-start

commit v3 on v2

--- a/solution.py
+++ b/solution.py
@@ -18,12 +18,13 @@
 LOW = -1e30
 CHUNK = 256
 SUB = 128
-DEPTH = 2
-BATCH = 4
+DEPTH = dict(z=2, l=2, y=2, h=2)
+BATCH = 6
 CHUNKS = 4
 SUBS = 4
-NEAR = (0, 1, 3, 6, 7)
-TUNE = dict(y_far=-0.23, y_col=0.99, h_dy=(14.71, 7.92, -16.21, 18.43), z_hop=-74.15, z_sub=-20.38, z_late=-48.75, l_hop=-29.58, l_sub=22.48, by_h=())
+H_CUT, W_CUT = 1, 1
+NEAR = (0, 2, 3, 5, 7)
+TUNE = dict(y_far=-19.62, y_col=1.26, h_dy=(-3.37, -10.43, 17.88, -1.79), z_hop=1.73, z_sub=-12.0, z_late=31.14, l_hop=-29.7, l_sub=7.34, by_h=(3,))
 
 
 def way_in(item):
@@ -31,9 +32,9 @@
         _, col, dy, j = item
         if col == 0:
             if dy == 2:
-                return "yp" if j < CHUNKS // 2 else "ym"
+                return "yp" if j < CHUNKS * W_CUT // 2 else "ym"
             return {0: None, 3: "yp", 1: "ym"}[dy]
-        if dy in (0, 2) or j in TUNE["by_h"]:
+        if dy in (0, 2) or j // W_CUT in TUNE["by_h"]:
             return "h"
         return "yp" if dy == 3 else "ym"
     _, who, dz, sub = item
@@ -42,7 +43,7 @@
     if who == 1 and dz in NEAR:
         return "l"
     if dz == 4:
-        return "zp" if sub < SUBS // 2 else "zm"
+        return "zp" if sub < SUBS * H_CUT // 2 else "zm"
     return "zp" if dz > 4 else "zm"
 
 
@@ -68,31 +69,31 @@
     if item[0] == "w":
         _, col, dy, j = item
         if link == "h":
-            return (j + t["h_dy"][dy], dy)
-        return (j + (t["y_far"] if dy else 0.0) + t["y_col"] * col, dy)
+            return (j / W_CUT + t["h_dy"][dy], dy)
+        return (j / W_CUT + (t["y_far"] if dy else 0.0) + t["y_col"] * col, dy)
     _, who, dz, sub = item
     hops = min(dz, 8 - dz)
     if link == "l":
-        return (hops * t["l_hop"] + sub * t["l_sub"], dz)
-    return (hops * t["z_hop"] + sub * t["z_sub"] + who * t["z_late"], dz)
+        return (hops * t["l_hop"] + sub / H_CUT * t["l_sub"], dz)
+    return (hops * t["z_hop"] + sub / H_CUT * t["z_sub"] + who * t["z_late"], dz)
 
 
 def plan():
-    wire = {"w": 2.85, "h": 1.43}
-    delay = 2.0
-    norm_time, jobs_time, unit_time = 0.45, 0.15, 0.4
+    wire = {"w": 2.85 / W_CUT, "h": 1.43 / H_CUT}
+    delay = 2.6
+    norm_time, jobs_time, unit_time = 0.35, 0.15, 0.38
     names = ("zp", "zm", "l", "yp", "ym", "h")
     free = dict.fromkeys(names, 0.0)
     ends = {n: [] for n in names}
     ready = {n: [] for n in names}
     arrivals, ops = [], []
-    for sub in range(SUBS):
-        heapq.heappush(arrivals, (0.0, ("h", 0, 0, sub)))
-    for j in range(CHUNKS):
-        heapq.heappush(arrivals, (1.0 + 0.2 * j, ("w", 0, 0, j)))
+    for piece in range(SUBS * H_CUT):
+        heapq.heappush(arrivals, (0.0, ("h", 0, 0, piece)))
+    for piece in range(CHUNKS * W_CUT):
+        heapq.heappush(arrivals, (1.0 + 0.2 * (piece // W_CUT), ("w", 0, 0, piece)))
     tokens = [(who, sub) for sub in range(SUBS) for who in (0, 1)]
-    missing = {("c", j): 8 for j in range(CHUNKS)}
-    missing.update({("n", *w): 8 for w in tokens})
+    missing = {("c", j): 8 * W_CUT for j in range(CHUNKS)}
+    missing.update({("n", *w): 8 * H_CUT for w in tokens})
     token_parts = {w: 2 for w in tokens}
     norms, units, chunks_here, tokens_here = [], [], [], []
     now = 0.0
@@ -100,7 +101,7 @@
     def top_up():
         for n in names:
             ends[n] = [e for e in ends[n] if e > now]
-            while ready[n] and len(ends[n]) < DEPTH:
+            while ready[n] and len(ends[n]) < DEPTH[n[0]]:
                 _, item = heapq.heappop(ready[n])
                 end = max(now, free[n]) + wire[item[0]]
                 free[n] = end
@@ -125,7 +126,7 @@
                 heapq.heappush(ready[n], (rank(n, item), item))
             if not arrivals or arrivals[0][0] > now:
                 top_up()
-            key = ("c", item[3]) if item[0] == "w" else ("n", item[1], item[3])
+            key = ("c", item[3] // W_CUT) if item[0] == "w" else ("n", item[1], item[3] // H_CUT)
             missing[key] -= 1
             if missing[key] == 0:
                 if key[0] == "c":
@@ -141,20 +142,22 @@
             part_of(who_sub)
             top_up()
         elif units:
-            batch = sorted(units[:BATCH])
-            del units[:BATCH]
+            units.sort(key=lambda unit: -unit[0])
+            batch = [u for u in units if u[0] == units[0][0]][:BATCH]
+            units = [u for u in units if u not in batch]
+            batch.sort()
             now += jobs_time + unit_time * len(batch)
             ops.append(("jobs", tuple(batch)))
             top_up()
         else:
             now = arrivals[0][0]
             top_up()
-    return ops, now
+    return ops
 
 
 def kernel(
     hidden, gain_in, weight, ids_in, lens, old_in, adv_in, roll_in, row,
-    logp_out, loss_out, sum_out,
+    out,
     w_all, hid, normed, ids, id_row, m_acc, s_acc, q_acc, p_acc,
     stat_rows, stat_quad, stat_all, ref_rows, ref_all, gains, tot_all, gain, old, adv, roll,
     local_sem, own_sem, wp_sem, w_sem, h_sem, n_sem, g_sem, all_sem, send_sem,
@@ -233,7 +236,7 @@
             ((gain_in, gain), (roll_in, roll), (ids_in, ids.at[0]), (old_in, old), (adv_in, adv))
         )
     ]
-    hid_in = pltpu.make_async_copy(hidden, hid.at[z], local_sem.at[5])
+    hid_in = pltpu.make_async_copy(hidden, hid.at[z], local_sem.at[7])
     hid_in.start()
     small[0].start()
     small[2].start()
@@ -259,7 +262,7 @@
     small[2].wait()
     pl.semaphore_wait(barrier, 8)
 
-    ops = plan()[0]
+    ops = plan()
     first_who, first_sub = next(op[1] for op in ops if op[0] == "norm")
     assert first_who == 0
 
@@ -351,6 +354,21 @@
                 line = jnp.where((line >= 0) & (line < cols), line, -(1 << 20))
                 id_row[:, pl.ds(place(s // 2, sub, (c + s) % 2), 128)] = line
 
+    def share(who):
+        tokens = slice(who * 2 * SUBS * SUB, (who + 1) * 2 * SUBS * SUB)
+        top = jnp.max(m_acc[:, tokens], axis=0, keepdims=True)
+        scale = jnp.exp(m_acc[:, tokens] - top)
+        total = jnp.sum(s_acc[:, tokens] * scale, axis=0, keepdims=True)
+        square = jnp.sum(q_acc[:, tokens] * (scale * scale), axis=0, keepdims=True)
+        chosen = jnp.sum(p_acc[:, tokens], axis=0, keepdims=True)
+        for core in (0, 1):
+            starts = [(sub * 2 + core) * SUB for sub in range(SUBS)]
+            stat_rows[who * 2 + (core + c) % 2] = jnp.concatenate(
+                [value[:, i : i + SUB] for value in (top, total, square, chosen) for i in starts], axis=0
+            )
+        for s in (2, 3) if who else (1,):
+            remote(stat_rows.at[s], stat_quad.at[s - 1], send_sem.at[9], all_sem.at[3], quad[s]).start()
+
     def to_plane(array, s, r):
         @pl.loop(0, 31)
         def _(i):
@@ -384,7 +402,7 @@
         remote(ids.at[0], ids.at[s], send_sem.at[8], all_sem.at[0], quad[s]).start()
     hid_in.wait()
 
-    batches = 0
+    batches, neighbours_left = 0, SUBS * CHUNKS
     extra = {1: ref_start, 4: ref_pick, 5: ref_send, 8: ref_wait}
     for number, op in enumerate(ops):
         if op[0] == "send":
@@ -396,25 +414,17 @@
         else:
             for unit in op[1]:
                 job(*unit)
+                neighbours_left -= unit[0]
+            if neighbours_left == 0:
+                share(1)
+                neighbours_left = -1
             batches += 1
             if batches in extra:
                 extra[batches]()
         if number == 40:
             ids_to_row()
 
-    top = jnp.max(m_acc[...], axis=0, keepdims=True)
-    scale = jnp.exp(m_acc[...] - top)
-    total = jnp.sum(s_acc[...] * scale, axis=0, keepdims=True)
-    square = jnp.sum(q_acc[...] * (scale * scale), axis=0, keepdims=True)
-    chosen = jnp.sum(p_acc[...], axis=0, keepdims=True)
-    for who in (0, 1):
-        for core in (0, 1):
-            starts = [((who * SUBS + sub) * 2 + core) * SUB for sub in range(SUBS)]
-            stat_rows[who * 2 + (core + c) % 2] = jnp.concatenate(
-                [value[:, i : i + SUB] for value in (top, total, square, chosen) for i in starts], axis=0
-            )
-    for s in range(1, 4):
-        remote(stat_rows.at[s], stat_quad.at[s - 1], send_sem.at[9], all_sem.at[3], quad[s]).start()
+    share(0)
     received(stat_quad, all_sem.at[3])
 
     def merge(parts):
@@ -430,8 +440,8 @@
     stat_all[0] = jnp.concatenate(merge([stat_rows[0], *(stat_quad[s] for s in range(3))]), axis=0)
 
     to_line(stat_all, 10, 4)
-    small[3].wait()
-    small[4].wait()
+    for k in (3, 4):
+        small[k].wait()
     all_received(stat_all, 4)
 
     top, total, square, chosen = merge([stat_all[k] for k in range(zs)])
@@ -477,8 +487,8 @@
     to_plane(tot_all, 11, 5)
 
     for b in range(blocks):
-        logp_out[:, b * 128 : (b + 1) * 128] = new_logp[b : b + 1, :]
-        loss_out[:, b * 128 : (b + 1) * 128] = token_loss[b : b + 1, :]
+        out[0:1, b * 128 : (b + 1) * 128] = new_logp[b : b + 1, :]
+        out[1:2, b * 128 : (b + 1) * 128] = token_loss[b : b + 1, :]
 
     def left(src, sem):
         remote(src, src, sem, local_sem.at[0], partner).wait_send()
@@ -506,7 +516,7 @@
     live_count, loss, kl, grads = [
         jnp.sum(jnp.where(lane == k, sums, 0.0), axis=1, keepdims=True) for k in range(4)
     ]
-    sum_out[...] = jnp.where(
+    out[2:3, 0:128] = jnp.where(
         lane == 0, loss / live_count, jnp.where(lane == 1, kl / live_count, jnp.sqrt(grads / live_count))
     )
     left(tot_all.at[0:31], send_sem.at[11])
@@ -517,20 +527,15 @@
     rows_dev, cols = head_weight.shape
     zs = lax.axis_size("tensor")
     depth = features * zs
-    vmem = pl.BlockSpec(memory_space=pltpu.VMEM)
-    smem = pl.BlockSpec(memory_space=pltpu.SMEM)
-    hbm = pl.BlockSpec(memory_space=pltpu.HBM)
+    hbm, smem = pl.BlockSpec(memory_space=pltpu.HBM), pl.BlockSpec(memory_space=pltpu.SMEM)
     f32, bf16, i32 = jnp.float32, jnp.bfloat16, jnp.int32
     dma = pltpu.SemaphoreType.DMA
-    new_logp, token_loss, summary = pl.pallas_call(
+    arrays = (hidden, norm_gain, head_weight.T, token_ids, lengths, old_logp, advantages, rollout_logp, rollout_row)
+    packed = pl.pallas_call(
         kernel,
-        out_shape=(
-            jax.ShapeDtypeStruct((1, tokens), f32),
-            jax.ShapeDtypeStruct((1, tokens), f32),
-            jax.ShapeDtypeStruct((1, 128), f32),
-        ),
-        in_specs=[hbm, hbm, hbm, hbm, smem, hbm, hbm, hbm, smem],
-        out_specs=(vmem, vmem, vmem),
+        out_shape=jax.ShapeDtypeStruct((8, tokens), f32),
+        in_specs=[smem if a.size == 1 else hbm for a in arrays],
+        out_specs=pl.BlockSpec(memory_space=pltpu.VMEM),
         scratch_shapes=[
             pltpu.VMEM((CHUNKS, CHUNK, depth), bf16),
             pltpu.VMEM((2 * zs, tokens, features), bf16),
@@ -549,7 +554,7 @@
             pltpu.VMEM((1, tokens), f32),
             pltpu.VMEM((1, tokens), f32),
             pltpu.VMEM((1, rollout_logp.shape[1]), f32),
-            dma((6,)),
+            dma((8,)),
             dma((CHUNKS,)),
             dma((CHUNKS,)),
             dma((8, CHUNKS)),
@@ -560,12 +565,12 @@
             dma((13,)),
         ],
         compiler_params=pltpu.CompilerParams(
-            collective_id=0, has_side_effects=True, vmem_limit_bytes=64 * 1024 * 1024 - 256 * 1024
+            collective_id=0, has_side_effects=True, vmem_limit_bytes=32 * 1024 * 1024
         ),
     )(
-        hidden, norm_gain, head_weight.T, token_ids, lengths, old_logp, advantages, rollout_logp, rollout_row
+        *(a if a.size == 1 else pltpu.with_memory_space_constraint(a, pltpu.HBM) for a in arrays)
     )
-    return new_logp, token_loss, summary[0, :3]
+    return packed[0:1], packed[1:2], packed[2, :3]
 
 
 def solution(mesh):

time: 72 us -> 66 us (0.917)
  Pallas kernels: 67.6 us -> 62.8 us
  local copies, waits for them, and re-layouts: 2.34 us -> 1.1 us
    pallas_call x1, Pallas kernels: 67.6 us -> 62.8 us  [shards(): pl.pallas_call(kernel, out_shape=jax.ShapeDtypeStruct((8, tokens), f32),...]
    unnamed x8 -> x0, local copies, waits for them, and re-layouts: 1.83 us -> none
where the time goes in v3:
time: 66 us; the launch traced here: 65.8 us
  Pallas kernels  62.8 us (95%)
  between operations  1.93 us (3%)
  local copies, waits for them, and re-layouts  1.1 us (2%)
    pallas_call x1, Pallas kernels, shards(): pl.pallas_call(kernel, out_shape=jax.ShapeDtypeStruct((8, tokens), f32),...  62.8 us

profile of v3, /device:TPU:1, one launch (start us, length us, event | category | flops | bytes accessed | tf_op | source)
XLA Modules:
  0.0 65.8 jit_solution(13552603073167081792)
XLA Ops:
  1.9 62.8 %shard_map.112 = f32[8,512]{1,0:T(8,128)S(1)} custom-call(bf16[512,256]{1,0:T(8,128)(2,1)} %hidden.1, bf16[256]{0:T(256)(128)(2,1)} %gain_in.1, bf16[4016,128]{1,0:T(8,128)(2,1)} %bitcast.3, s32[1,512]{1,0:T(1,128)} %ids_in.1, s32[1]{0:T(128)S(6)} %copy.12.lens, f32[1,512]{1,0:T(1,128)} %old_in.1, f32[1,512]{1,0:T(1,128)} %adv_in.1, f32[1,64]{1,0:T(1,128)} %roll_in.1, ...), custom_call_target="tpu_custom_call" | custom-call | tf_op jit(solution)/shard_map/pallas_call | solution.py:534
  64.7 0.6 fusion
  65.3 0.5 slice_bitcast_fusion

commit v4 on v3

--- a/solution.py
+++ b/solution.py
@@ -80,7 +80,7 @@
 
 def plan():
     wire = {"w": 2.85 / W_CUT, "h": 1.43 / H_CUT}
-    delay = 2.6
+    delay = 2.3
     norm_time, jobs_time, unit_time = 0.35, 0.15, 0.38
     names = ("zp", "zm", "l", "yp", "ym", "h")
     free = dict.fromkeys(names, 0.0)
@@ -160,7 +160,7 @@
     out,
     w_all, hid, normed, ids, id_row, m_acc, s_acc, q_acc, p_acc,
     stat_rows, stat_quad, stat_all, ref_rows, ref_all, gains, tot_all, gain, old, adv, roll,
-    local_sem, own_sem, wp_sem, w_sem, h_sem, n_sem, g_sem, all_sem, send_sem,
+    local_sem, own_sem, wp_sem, w_sem, h_sem, n_sem, g_sem, all_sem, send_sem, round_sem,
 ):
     lo, f, z = lax.axis_index("dp"), lax.axis_index("fsdp"), lax.axis_index("tensor")
     hi, y, c = f // 8, (f // 2) % 4, f % 2
@@ -188,11 +188,11 @@
     }
 
     def plane_peer(k):
-        other = (me + k) % 32
-        return {"dp": other // 16, "fsdp": other % 16, "tensor": z}
+        other = lax.rem(me + k, 32)
+        return {"dp": lax.div(other, 16), "fsdp": lax.rem(other, 16), "tensor": z}
 
     def line_peer(k):
-        return {"dp": lo, "fsdp": f, "tensor": (z + k) % zs}
+        return {"dp": lo, "fsdp": f, "tensor": lax.rem(z + k, zs)}
 
     def remote(src, dst, s, r, device):
         return pltpu.make_async_remote_copy(
@@ -268,14 +268,17 @@
 
     def w_piece(col, dy, j):
         g = (1 - hi if col else hi) * 4 + (y + dy) % 4
-        return w_all.at[j, :, pl.ds(pl.multiple_of(g * 256, 256), 256)], w_sem.at[g, j]
+        rows = CHUNK // W_CUT
+        part = w_all.at[j // W_CUT, pl.ds(j % W_CUT * rows, rows), pl.ds(pl.multiple_of(g * 256, 256), 256)]
+        return part, w_sem.at[g, j]
 
     def h_piece(who, dz, sub):
         owner = who * zs + (z + dz) % zs
-        return hid.at[owner, pl.ds(sub * SUB, SUB), :], h_sem.at[owner, sub]
+        rows = SUB // H_CUT
+        return hid.at[owner, pl.ds(sub * rows, rows), :], h_sem.at[owner, sub]
 
     def with_gain(link, item):
-        return link[0] == "z" and item[1] == 0 and item[3] == first_sub
+        return link[0] == "z" and item[1] == 0 and item[3] == first_sub * H_CUT
 
     def send(link, item):
         if item[0] == "w":
@@ -296,14 +299,16 @@
         if item[0] == "p":
             received(normed.at[pl.ds(place(*item[1:], 1 - c), SUB), :], n_sem.at[item[1], item[2]])
         elif item[0] == "w" and item[1:3] == (0, 0):
-            j = item[3]
+            if item[3] % W_CUT:
+                return
+            j = item[3] // W_CUT
             sized(j, quarter, lambda n: own_weights(j, n).wait())
             sized(j, quarter, lambda n: received(w_all.at[j, pl.ds(0, n), pl.ds(lane0, 128)], wp_sem.at[j]))
         elif item[0] == "w":
             received(*w_piece(*item[1:]))
         elif item[1:3] != (0, 0):
             received(*h_piece(*item[1:]))
-            if item[1] == 0 and item[3] == first_sub:
+            if item[1] == 0 and item[3] == first_sub * H_CUT:
                 k = (z + item[2]) % zs
                 received(gains.at[k], g_sem.at[k])
 
@@ -325,16 +330,20 @@
         ref = normed.at[pl.ds(place(who, sub, c), SUB), :]
         remote(ref, ref, send_sem.at[5], n_sem.at[who, sub], partner).start()
 
-    def job(who, sub, j):
+    def job(who, sub, j, count):
         base = (quarter * CHUNKS + j) * CHUNK
+        rows = count * CHUNK
         start = (who * SUBS + sub) * 2 * SUB
         tokens = slice(start, start + 2 * SUB)
         logits = lax.dot_general(
-            w_all[j], normed[tokens, :], (((1,), (1,)), ((), ())), preferred_element_type=jnp.float32
-        ).reshape(CHUNK // 8, 8, 2 * SUB)
-        shape = (CHUNK // 8, 8, 1)
+            w_all[j : j + count].reshape(rows, w_all.shape[2]),
+            normed[tokens, :],
+            (((1,), (1,)), ((), ())),
+            preferred_element_type=jnp.float32,
+        ).reshape(rows // 8, 8, 2 * SUB)
+        shape = (rows // 8, 8, 1)
         column = lax.broadcasted_iota(jnp.int32, shape, 0) * 8 + lax.broadcasted_iota(jnp.int32, shape, 1)
-        if j == CHUNKS - 1:
+        if j + count == CHUNKS:
             logits = jnp.where(column < cols - base, logits, LOW)
         wanted = (id_row[:, tokens] - base)[None]
         p_acc[:, tokens] += jnp.sum(jnp.where(column == wanted, logits, 0.0), axis=0)
@@ -372,7 +381,7 @@
     def to_plane(array, s, r):
         @pl.loop(0, 31)
         def _(i):
-            k = (i + 15) % 31 + 1
+            k = lax.rem(i + 15, 31) + 1
             remote(array.at[0], array.at[k], send_sem.at[s], all_sem.at[r], plane_peer(k)).start()
 
     def to_line(array, s, r):
@@ -381,6 +390,16 @@
 
     def all_received(array, r):
         received(array.at[1:], all_sem.at[r])
+
+    rounds = []
+
+    def tell():
+        rounds.append(len(rounds))
+        for n in ("yp", "ym", "h"):
+            pl.semaphore_signal(round_sem.at[rounds[-1]], inc=1, device_id=target[n], device_id_type=MESH)
+
+    def hear():
+        pl.semaphore_wait(round_sem.at[rounds[-1]], 3)
 
     def ref_start():
         to_plane(ref_rows, 6, 1)
@@ -403,7 +422,10 @@
     hid_in.wait()
 
     batches, neighbours_left = 0, SUBS * CHUNKS
-    extra = {1: ref_start, 4: ref_pick, 5: ref_send, 8: ref_wait}
+    extra = {8: ref_wait}
+    first_norm = next(number for number, op in enumerate(ops) if op[0] == "norm")
+    early = {25: tell, 40: hear, 41: tell, 60: hear, 61: tell, 85: hear, 86: ref_start}
+    early.update({first_norm - 1: ref_pick, first_norm: ref_send})
     for number, op in enumerate(ops):
         if op[0] == "send":
             send(op[1], op[2])
@@ -412,9 +434,14 @@
         elif op[0] == "norm":
             normalize(*op[1])
         else:
-            for unit in op[1]:
-                job(*unit)
-                neighbours_left -= unit[0]
+            for who, sub, j in op[1]:
+                if (who, sub, j - 1) in op[1]:
+                    continue
+                count = 1
+                while (who, sub, j + count) in op[1]:
+                    count += 1
+                job(who, sub, j, count)
+            neighbours_left -= sum(unit[0] for unit in op[1])
             if neighbours_left == 0:
                 share(1)
                 neighbours_left = -1
@@ -423,6 +450,8 @@
                 extra[batches]()
         if number == 40:
             ids_to_row()
+        if number in early:
+            early[number]()
 
     share(0)
     received(stat_quad, all_sem.at[3])
@@ -499,9 +528,9 @@
         op[1] if op[1] in ("l", "zp", "zm") else "w" for op in ops if op[0] == "send"
     )
     count["g"] = sum(op[0] == "send" and with_gain(op[1], op[2]) for op in ops)
-    left(w_all.at[:, :, 0 : count["w"] // CHUNKS * 256], send_sem.at[1])
-    left(hid.at[0 : count["l"] // SUBS], send_sem.at[2])
-    left(hid.at[0 : (count["zp"] + count["zm"]) // SUBS], send_sem.at[3])
+    left(w_all.at[:, :, 0 : count["w"] // (CHUNKS * W_CUT) * 256], send_sem.at[1])
+    left(hid.at[0 : count["l"] // (SUBS * H_CUT)], send_sem.at[2])
+    left(hid.at[0 : (count["zp"] + count["zm"]) // (SUBS * H_CUT)], send_sem.at[3])
     left(gains.at[0 : count["g"]], send_sem.at[4])
     left(normed.at[0 : 2 * SUBS * SUB, :], send_sem.at[5])
     left(ref_rows.at[0:31], send_sem.at[6])
@@ -557,12 +586,13 @@
             dma((8,)),
             dma((CHUNKS,)),
             dma((CHUNKS,)),
-            dma((8, CHUNKS)),
-            dma((2 * zs, SUBS)),
+            dma((8, CHUNKS * W_CUT)),
+            dma((2 * zs, SUBS * H_CUT)),
             dma((2, SUBS)),
             dma((zs,)),
             dma((6,)),
             dma((13,)),
+            pltpu.SemaphoreType.REGULAR((3,)),
         ],
         compiler_params=pltpu.CompilerParams(
             collective_id=0, has_side_effects=True, vmem_limit_bytes=32 * 1024 * 1024

time: 66 us -> 64.8 us (0.982)
  Pallas kernels: 62.8 us -> 61.7 us
    pallas_call x1, Pallas kernels: 62.8 us -> 61.7 us  [shards(): pl.pallas_call(kernel, out_shape=jax.ShapeDtypeStruct((8, tokens), f32),...]
where the time goes in v4:
time: 64.8 us; the launch traced here: 64.7 us
  Pallas kernels  61.7 us (95%)
  between operations  1.93 us (3%)
  local copies, waits for them, and re-layouts  1.1 us (2%)
    pallas_call x1, Pallas kernels, shards(): pl.pallas_call(kernel, out_shape=jax.ShapeDtypeStruct((8, tokens), f32),...  61.7 us

profile of v4, /device:TPU:1, one launch (start us, length us, event | category | flops | bytes accessed | tf_op | source)
XLA Modules:
  0.0 64.7 jit_solution(16103728900011615850)
XLA Ops:
  1.9 61.7 %shard_map.112 = f32[8,512]{1,0:T(8,128)S(1)} custom-call(bf16[512,256]{1,0:T(8,128)(2,1)} %hidden.1, bf16[256]{0:T(256)(128)(2,1)} %gain_in.1, bf16[4016,128]{1,0:T(8,128)(2,1)} %bitcast.3, s32[1,512]{1,0:T(1,128)} %ids_in.1, s32[1]{0:T(128)S(6)} %copy.12.lens, f32[1,512]{1,0:T(1,128)} %old_in.1, f32[1,512]{1,0:T(1,128)} %adv_in.1, f32[1,64]{1,0:T(1,128)} %roll_in.1, ...), custom_call_target="tpu_custom_call" | custom-call | tf_op jit(solution)/shard_map/pallas_call | solution.py:563
  63.6 0.6 fusion
  64.2 0.5 slice_bitcast_fusion

commit v5 on v4

--- a/solution.py
+++ b/solution.py
@@ -155,6 +155,21 @@
     return ops
 
 
+def tidy(ops):
+    out, held = [], ()
+    for op in ops:
+        if op[0] == "jobs":
+            if len(op[1]) == 1 and out[-1][0] == "jobs":
+                out[-1] = ("jobs", out[-1][1] + op[1])
+                continue
+            held += op[1]
+            if len(held) == 1:
+                continue
+            op, held = ("jobs", held), ()
+        out.append(op)
+    return out + [("jobs", held)] * bool(held)
+
+
 def kernel(
     hidden, gain_in, weight, ids_in, lens, old_in, adv_in, roll_in, row,
     out,
@@ -262,7 +277,7 @@
     small[2].wait()
     pl.semaphore_wait(barrier, 8)
 
-    ops = plan()
+    ops = tidy(plan())
     first_who, first_sub = next(op[1] for op in ops if op[0] == "norm")
     assert first_who == 0
 
@@ -330,20 +345,16 @@
         ref = normed.at[pl.ds(place(who, sub, c), SUB), :]
         remote(ref, ref, send_sem.at[5], n_sem.at[who, sub], partner).start()
 
-    def job(who, sub, j, count):
+    def job(who, sub, j):
         base = (quarter * CHUNKS + j) * CHUNK
-        rows = count * CHUNK
         start = (who * SUBS + sub) * 2 * SUB
         tokens = slice(start, start + 2 * SUB)
         logits = lax.dot_general(
-            w_all[j : j + count].reshape(rows, w_all.shape[2]),
-            normed[tokens, :],
-            (((1,), (1,)), ((), ())),
-            preferred_element_type=jnp.float32,
-        ).reshape(rows // 8, 8, 2 * SUB)
-        shape = (rows // 8, 8, 1)
+            w_all[j], normed[tokens, :], (((1,), (1,)), ((), ())), preferred_element_type=jnp.float32
+        ).reshape(CHUNK // 8, 8, 2 * SUB)
+        shape = (CHUNK // 8, 8, 1)
         column = lax.broadcasted_iota(jnp.int32, shape, 0) * 8 + lax.broadcasted_iota(jnp.int32, shape, 1)
-        if j + count == CHUNKS:
+        if j == CHUNKS - 1:
             logits = jnp.where(column < cols - base, logits, LOW)
         wanted = (id_row[:, tokens] - base)[None]
         p_acc[:, tokens] += jnp.sum(jnp.where(column == wanted, logits, 0.0), axis=0)
@@ -434,13 +445,8 @@
         elif op[0] == "norm":
             normalize(*op[1])
         else:
-            for who, sub, j in op[1]:
-                if (who, sub, j - 1) in op[1]:
-                    continue
-                count = 1
-                while (who, sub, j + count) in op[1]:
-                    count += 1
-                job(who, sub, j, count)
+            for unit in op[1]:
+                job(*unit)
             neighbours_left -= sum(unit[0] for unit in op[1])
             if neighbours_left == 0:
                 share(1)

time: 64.8 us -> 64.2 us (level)
  no operation moved by 1% of the time
where the time goes in v5:
time: 64.2 us; the launch traced here: 64.1 us
  Pallas kernels  61.1 us (95%)
  between operations  1.93 us (3%)
  local copies, waits for them, and re-layouts  1.1 us (2%)
    pallas_call x1, Pallas kernels, shards(): pl.pallas_call(kernel, out_shape=jax.ShapeDtypeStruct((8, tokens), f32),...  61.1 us

profile of v5, /device:TPU:1, one launch (start us, length us, event | category | flops | bytes accessed | tf_op | source)
XLA Modules:
  0.0 64.1 jit_solution(15768997118157345989)
XLA Ops:
  1.9 61.1 %shard_map.112 = f32[8,512]{1,0:T(8,128)S(1)} custom-call(bf16[512,256]{1,0:T(8,128)(2,1)} %hidden.1, bf16[256]{0:T(256)(128)(2,1)} %gain_in.1, bf16[4016,128]{1,0:T(8,128)(2,1)} %bitcast.3, s32[1,512]{1,0:T(1,128)} %ids_in.1, s32[1]{0:T(128)S(6)} %copy.12.lens, f32[1,512]{1,0:T(1,128)} %old_in.1, f32[1,512]{1,0:T(1,128)} %adv_in.1, f32[1,64]{1,0:T(1,128)} %roll_in.1, ...), custom_call_target="tpu_custom_call" | custom-call | tf_op jit(solution)/shard_map/pallas_call | solution.py:569
  63.0 0.6 fusion
  63.6 0.5 slice_bitcast_fusion

commit v6 on v5

--- a/solution.py
+++ b/solution.py
@@ -155,19 +155,25 @@
     return ops
 
 
-def tidy(ops):
-    out, held = [], ()
+def late_waits(ops):
+    out, pending = [], collections.defaultdict(list)
     for op in ops:
-        if op[0] == "jobs":
-            if len(op[1]) == 1 and out[-1][0] == "jobs":
-                out[-1] = ("jobs", out[-1][1] + op[1])
+        needs = []
+        if op[0] == "wait":
+            item = op[1]
+            if item[0] == "p" or not links_of(item):
+                key = ("w", item[3]) if item[0] == "w" else (item[0], item[1], item[-1])
+                pending[key].append(op)
                 continue
-            held += op[1]
-            if len(held) == 1:
-                continue
-            op, held = ("jobs", held), ()
+        elif op[0] == "norm":
+            needs = [("h", *op[1])]
+        elif op[0] == "jobs":
+            needs = [key for unit in op[1] for key in (("p", *unit[:2]), ("w", unit[2]))]
+        for key in needs:
+            out.extend(pending.pop(key, ()))
         out.append(op)
-    return out + [("jobs", held)] * bool(held)
+    assert not any(pending.values())
+    return out
 
 
 def kernel(
@@ -277,7 +283,7 @@
     small[2].wait()
     pl.semaphore_wait(barrier, 8)
 
-    ops = tidy(plan())
+    ops = late_waits(plan())
     first_who, first_sub = next(op[1] for op in ops if op[0] == "norm")
     assert first_who == 0
 

time: 64.2 us -> 64 us (level)
  no operation moved by 1% of the time
where the time goes in v6:
time: 64 us; the launch traced here: 63.8 us
  Pallas kernels  60.8 us (95%)
  between operations  1.93 us (3%)
  local copies, waits for them, and re-layouts  1.1 us (2%)
    pallas_call x1, Pallas kernels, shards(): pl.pallas_call(kernel, out_shape=jax.ShapeDtypeStruct((8, tokens), f32),...  60.8 us

profile of v6, /device:TPU:1, one launch (start us, length us, event | category | flops | bytes accessed | tf_op | source)
XLA Modules:
  0.0 63.8 jit_solution(8929264544727712888)
XLA Ops:
  1.9 60.8 %shard_map.112 = f32[8,512]{1,0:T(8,128)S(1)} custom-call(bf16[512,256]{1,0:T(8,128)(2,1)} %hidden.1, bf16[256]{0:T(256)(128)(2,1)} %gain_in.1, bf16[4016,128]{1,0:T(8,128)(2,1)} %bitcast.3, s32[1,512]{1,0:T(1,128)} %ids_in.1, s32[1]{0:T(128)S(6)} %copy.12.lens, f32[1,512]{1,0:T(1,128)} %old_in.1, f32[1,512]{1,0:T(1,128)} %adv_in.1, f32[1,64]{1,0:T(1,128)} %roll_in.1, ...), custom_call_target="tpu_custom_call" | custom-call | tf_op jit(solution)/shard_map/pallas_call | solution.py:575
  62.7 0.6 fusion
  63.3 0.5 slice_bitcast_fusion
